TPU v7x, 32 devices: a whole 2x2x4 slice. The times are simulated.
32 devices in a mesh: group: 2 (over x), patch: 16 (over z, y, core).
Axes of the slice: x: 2, y: 2, z: 4, core: 2. Of those that a mesh axis runs over, the one named last changes fastest.
Arguments:
- features: bfloat16 [32, 64, 4, 2304], P(('group', 'patch')), parts along dimension 0, may hold values from -6 to 6
- w_in: bfloat16 [28, 64], replicated, may hold values from -0.75 to 0.75
- w_plane: bfloat16 [9, 28, 28], replicated, may hold values from -0.375 to 0.375
- w_depth: bfloat16 [3, 28, 28], replicated, may hold values from -0.625 to 0.625
- w_head: bfloat16 [3, 28], replicated, may hold values from -1 to 1
- brick_owner: int32 [32], P(('group', 'patch')), parts along dimension 0, may hold values from 0 to 15, each once
- patch_anchor: int32 [32], P(('group', 'patch')), parts along dimension 0, may hold values from 0 to 3, as said below
- aug_code: int32 [32], P(('group', 'patch')), parts along dimension 0, may hold values from 0 to 7, as said below
Outputs:
- blended: float32 [32, 4, 2304], P(('group', 'patch')), parts along dimension 0
There are 2 independent parts, one for each index of `group`. A program takes and returns all parts, laid end to end along the dimension named above; an argument that names none is the same for every part. Nothing has to cross between parts.
Inputs may be any that keep to these rules, and one draw needn't show every extreme that they name: `brick_owner`: every device owns exactly one brick of its region. `patch_anchor`: devices 8 k to 8 k + 7 share one anchor; different positions have different anchors. `aug_code`: devices 8 k to 8 k + 7 hold each code once.
All inputs are finite; a program needn't handle non-finite values.
Results may differ from a plain program's by a relative error of at most 0.00048.
Values sent between devices are 32-bit elements; how exact they have to be, the bound alone decides.
No kernel may reach another device: no remote copies, remote signals or barrier semaphores. Data moves between devices by JAX's collectives and lax.ppermute only.
A program may use at most 64 MiB of HBM per device.

v0:
```python
import functools
import math

import numpy as np

import jax
import jax.numpy as jnp
from jax import lax
from jax.experimental import pallas as pl
from jax.experimental.pallas import tpu as pltpu
from jax.sharding import PartitionSpec as P


F32 = jnp.float32
BF16 = jnp.bfloat16
I32 = jnp.int32
PAD = 32
LANES = 128
CHUNKS = 2
FAR_FIRST = (3, 2, 1)
DIRECT = 2
LEAD = 1
SPARE = 96


def iota(shape, axis):
    return lax.broadcasted_iota(I32, shape, axis)


def vmem():
    return pl.BlockSpec(memory_space=pltpu.VMEM)


def smem():
    return pl.BlockSpec(memory_space=pltpu.SMEM)


def hbm():
    return pl.BlockSpec(memory_space=pltpu.HBM)


def stay(*arrays):
    return [pltpu.with_memory_space_constraint(a, pltpu.HBM) for a in arrays]


def params():
    return pltpu.CompilerParams(vmem_limit_bytes=16 * 2**20)


def cost(flops):
    return pl.CostEstimate(flops=flops, bytes_accessed=2**20, transcendentals=0)


def bump(length):
    position = (np.arange(length, dtype=np.float64) + 0.5) / length
    return 0.1 + np.sin(np.pi * position) ** 2


def front_kernel(aug_ref, w_in_hbm, w_plane_hbm, w_depth_hbm, w_head_hbm, x_hbm, plane_ref, depth_ref, head_ref, xs_ref, w_in_ref, w_plane_ref, w_depth_ref, w_head_ref, x_ref, big_ref, plane_scr, depth_scr, sems):
    size = x_hbm.shape[2] // CHUNKS
    feats = [
        pltpu.make_async_copy(x_hbm.at[:, :, pl.ds(c * size, size)], x_ref.at[:, :, pl.ds(c * size, size)], sems.at[4 + c])
        for c in range(CHUNKS)
    ]
    pairs = ((w_plane_hbm, w_plane_ref), (w_in_hbm, w_in_ref), (w_depth_hbm, w_depth_ref), (w_head_hbm, w_head_ref))
    copies = [pltpu.make_async_copy(src, dst, sems.at[k]) for k, (src, dst) in enumerate(pairs)]
    for copy in copies + feats:
        copy.start()
    for copy in copies:
        copy.wait()
    hidden, _ = w_in_ref.shape
    depth = depth_ref.shape[0] // PAD
    maps = w_head_ref.shape[0]
    aug = aug_ref[0]
    zf, yf, xf = aug & 1, (aug >> 1) & 1, (aug >> 2) & 1

    rows, cols = big_ref.shape
    spread = (iota((rows, hidden), 0) % PAD == iota((rows, hidden), 1)).astype(BF16)
    gather = (iota((w_in_ref.shape[1], cols), 1) // depth == iota((w_in_ref.shape[1], cols), 0)).astype(BF16)
    tall = jnp.dot(spread, w_in_ref[...], preferred_element_type=F32).astype(BF16)
    wide = jnp.dot(tall, gather, preferred_element_type=F32)
    same = iota((rows, cols), 1) % depth == iota((rows, cols), 0) // PAD
    big_ref[...] = jnp.where(same, wide, 0.0).astype(BF16)

    plane_scr[...] = jnp.zeros_like(plane_scr)
    taps = [w_plane_ref[t].astype(F32) for t in range(9)]
    near = (((0,), (1, 2), ()), ((), (0, 1), (2,)))
    for py in range(2):
        for px in range(2):
            for dy in range(2):
                for dx in range(3):
                    hit = [taps[3 * ty + tx] for ty in near[py][dy + py] for tx in near[px][dx]]
                    if not hit:
                        continue
                    total = functools.reduce(lambda a, b: a + b, hit)
                    high = total.astype(BF16).astype(F32)
                    col = (3 * dy + dx) * PAD
                    plane_scr[py, pl.ds(px * PAD, hidden), pl.ds(col, hidden)] = high
                    plane_scr[py, pl.ds((2 + px) * PAD, hidden), pl.ds(col, hidden)] = total - high
    plane_ref[...] = plane_scr[...].astype(BF16)

    depth_scr[...] = jnp.zeros_like(depth_scr)
    for t in range(3):
        tap = w_depth_ref[t].astype(F32)
        for z in range(depth):
            if 0 <= z + t - 1 < depth:
                depth_scr[pl.ds(z * PAD, hidden), pl.ds((z + t - 1) * PAD, hidden)] = tap
    depth_ref[...] = depth_scr[...].astype(BF16)

    rows, cols = head_ref.shape
    pick = (iota((rows, maps), 0) % maps == iota((rows, maps), 1)).astype(BF16)
    tall = jnp.dot(pick, w_head_ref[...], preferred_element_type=F32).astype(BF16)
    gather = (iota((hidden, cols), 1) % PAD == iota((hidden, cols), 0)).astype(BF16)
    wide = jnp.dot(tall, gather, preferred_element_type=F32)
    at = iota((rows, cols), 0) // maps
    came = iota((rows, cols), 1) // PAD
    flip = (2 * yf + xf) * depth + (depth - 1) * zf
    head_ref[...] = jnp.where(at == (came ^ flip), wide, 0.0).astype(BF16)

    channels, depth, cells = x_ref.shape
    zeros = jnp.zeros((depth * PAD, LANES), BF16)
    xs_ref[:, pl.ds(0, LANES)] = zeros
    xs_ref[:, pl.ds(LANES + cells, LANES)] = zeros
    for c, copy in enumerate(feats):
        part = pl.ds(c * size, size)
        copy.wait()
        x = x_ref[:, :, part].reshape(channels * depth, size)
        xs_ref[:, pl.ds(LANES + c * size, size)] = jnp.dot(big_ref[...], x, preferred_element_type=F32).astype(BF16)


def front(aug_code, w_in, w_plane, w_depth, w_head, feat):
    _, channels = w_in.shape
    maps = w_head.shape[0]
    _, depth, cells = feat.shape
    plane = (2, 4 * PAD, 6 * PAD)
    depth_w = (depth * PAD, depth * PAD)
    head = (4 * depth * maps, 4 * depth * PAD)
    padded = (depth * PAD, cells + 2 * LANES)
    return pl.pallas_call(
        front_kernel,
        out_shape=[jax.ShapeDtypeStruct(s, BF16) for s in (plane, depth_w, head, padded)],
        in_specs=[smem()] + [hbm()] * 5,
        out_specs=[vmem()] * 4,
        scratch_shapes=[
            pltpu.VMEM(w_in.shape, BF16),
            pltpu.VMEM(w_plane.shape, BF16),
            pltpu.VMEM(w_depth.shape, BF16),
            pltpu.VMEM(w_head.shape, BF16),
            pltpu.VMEM(feat.shape, BF16),
            pltpu.VMEM((depth * PAD, channels * depth), BF16),
            pltpu.VMEM(plane, F32),
            pltpu.VMEM(depth_w, F32),
            pltpu.SemaphoreType.DMA((4 + CHUNKS,)),
        ],
        compiler_params=params(),
        cost_estimate=cost(10**8),
        name="front",
    )(aug_code, *stay(w_in, w_plane, w_depth, w_head, feat))


def patch_kernel(half, tiles, brick_rows, keep_from, last, aug_ref, xs_ref, plane_ref, depth_ref, head_ref, *refs):
    if last:
        carry_in, _, anchor_ref, out_ref, anchor_out, a_ref = refs
        anchor_out[...] = jnp.full(anchor_out.shape, anchor_ref[0], I32)
    else:
        out_ref, carry_out, a_ref = refs
    rows, _ = xs_ref.shape
    depth = rows // PAD
    step = 2 * LANES
    margin = LANES
    carried = carry_in.shape[0] if last else 0
    first_tile = tiles[0] * (step // LANES) - carried
    if last:
        a_ref[pl.ds(0, carried)] = carry_in[...]

    def window_stage(t):
        column = (iota((rows, step), 1) + t * step) % half
        block = xs_ref[:, pl.ds(t * step, step + 2 * margin)]
        near = []
        for d in (-1, 0, 1):
            near.append([])
            for e in (-1, 0, 1):
                at = margin + half * e + d
                one = lax.slice_in_dim(block, at, at + step, axis=1)
                if d:
                    one = jnp.where(column == (0 if d < 0 else half - 1), jnp.zeros_like(one), one)
                near[-1].append(one)
        return near

    def plane_stage(near, z):
        cut = slice(z * PAD, (z + 1) * PAD)
        centre = near[1][1][cut].astype(F32)
        first = []
        for py in range(2):
            around = jnp.concatenate([near[d][py + e][cut] for e in range(2) for d in range(3)], axis=0)
            mix = jnp.dot(plane_ref[py], around, preferred_element_type=F32)
            for px in range(2):
                total = mix[px * PAD : (px + 1) * PAD] + mix[(2 + px) * PAD : (3 + px) * PAD]
                first.append((centre + jnp.maximum(total, 0.0)).astype(BF16))
        return first

    def depth_stage(first, p):
        one = jnp.concatenate([first[z][p] for z in range(depth)], axis=0)
        mix = jnp.dot(depth_ref[...], one, preferred_element_type=F32)
        return (one.astype(F32) + jnp.maximum(mix, 0.0)).astype(BF16)

    def head_stage(t, second):
        logits = jnp.zeros((head_ref.shape[0], step), F32)
        for q in range(2):
            pair = jnp.concatenate(second[2 * q : 2 * q + 2], axis=0)
            logits = logits + jnp.dot(head_ref[:, 2 * q * rows : 2 * (q + 1) * rows], pair, preferred_element_type=F32)
        affinity = jax.nn.sigmoid(logits)
        for u in range(step // LANES):
            a_ref[t * (step // LANES) + u - first_tile] = affinity[:, u * LANES : (u + 1) * LANES]

    aug = aug_ref[0]
    yf, xf = (aug >> 1) & 1, (aug >> 2) & 1
    side = half // 4
    tail = side * side - LANES
    row_tiles = head_ref.shape[0] // 8
    lane = iota((8, LANES), 1)
    group = lane // tail
    span = -(-side * half // LANES)
    near_tiles = span - 2

    def source(cell, j, odd):
        y = cell // side
        x = cell - y * side
        y = jnp.where(yf == 1, side - 1 - y, y)
        x = jnp.where(xf == 1, side - 1 - x, x)
        return y * half + side * j + x + odd * (LANES // 2)

    def cut_stage(i, j):
        odd = i % 2
        owned = []
        for k in range(span):
            x = (lane + k * LANES + half - odd * (LANES // 2) % half) % half
            owned.append((x >= side * j) & (x < side * (j + 1)))
        src = source(lane, j, odd)
        main_lane, main_near = src % LANES, src < near_tiles * LANES
        rest_lane = source(LANES + lane % tail, j, odd) % LANES
        base = side * half * i // LANES - first_tile
        brick = (i ^ (3 * yf)) * 4 + (j ^ (3 * xf))
        packed = jnp.zeros((8, LANES), F32)
        for r in range(row_tiles):
            cut = pl.ds(8 * r, 8)
            merged = []
            for tiles_of in (range(near_tiles), range(near_tiles, span)):
                one = a_ref[base + tiles_of[0], cut]
                for k in tiles_of[1:]:
                    one = jnp.where(owned[k], a_ref[base + k, cut], one)
                merged.append(one)
            low = jnp.take_along_axis(merged[0], main_lane, axis=1)
            high = jnp.take_along_axis(merged[1], main_lane, axis=1)
            out_ref[brick, cut] = jnp.where(main_near, low, high)
            rest = jnp.take_along_axis(jnp.where(yf == 1, merged[0], merged[1]), rest_lane, axis=1)
            packed = jnp.where(group == r, rest, packed)
        out_ref[brick, pl.ds(8 * row_tiles, 8)] = packed

    first, second = {}, {}
    waiting = [(i, j) for i in brick_rows for j in range(4)]
    done = first_tile + carried
    for k in range(len(tiles) + 2):
        if k < len(tiles):
            near = window_stage(tiles[k])
            first[k] = []
        second[k - 1] = []
        for q in range(4):
            if k < len(tiles) and q < depth:
                first[k].append(plane_stage(near, q))
            if 0 <= k - 1 < len(tiles):
                second[k - 1].append(depth_stage(first[k - 1], q))
            if waiting and done >= side * half * waiting[0][0] // LANES + span:
                cut_stage(*waiting.pop(0))
        if 0 <= k - 2 < len(tiles):
            head_stage(tiles[k - 2], second[k - 2])
            done += step // LANES
    for left in waiting:
        cut_stage(*left)
    if not last:
        carry_out[...] = a_ref[pl.ds(keep_from - first_tile, done - keep_from)]


def patch_half(half, tiles, brick_rows, keep_from, last, aug_code, shifted, plane, depth_w, head, extra=()):
    kept = head.shape[0]
    carried = extra[0].shape[0] if last else 0
    bricks = jax.ShapeDtypeStruct((16, kept + 8, LANES), F32)
    beside = jax.ShapeDtypeStruct((1, LANES), I32) if last else jax.ShapeDtypeStruct((2 * len(tiles) - keep_from, kept, LANES), F32)
    spaces = [vmem(), vmem(), smem()] if last else []
    return pl.pallas_call(
        functools.partial(patch_kernel, half, tiles, brick_rows, keep_from, last),
        out_shape=[bricks, beside],
        in_specs=[smem()] + [vmem()] * 4 + spaces,
        out_specs=[vmem()] * 2,
        scratch_shapes=[pltpu.VMEM((2 * len(tiles) + carried, kept, LANES), F32)],
        input_output_aliases={6: 0} if last else {},
        compiler_params=params(),
        cost_estimate=cost(10**9),
    )(aug_code, shifted, plane, depth_w, head, *extra)


def seed_kernel(owner_ref, out_ref):
    here = iota(out_ref.shape, 1) == lax.axis_index("patch")
    out_ref[...] = jnp.where(here, owner_ref[0], 0)


def seed_table(owner, devices):
    width = -(-devices // LANES) * LANES
    return pl.pallas_call(
        seed_kernel,
        out_shape=jax.ShapeDtypeStruct((1, width), I32),
        in_specs=[smem()],
        out_specs=vmem(),
        compiler_params=params(),
        name="seed",
    )(owner)


def partner(devices, bit):
    return [(d, d ^ bit) for d in range(devices)]


def slots_kernel(devices, masks, table_ref, anchor_ref, mine_ref, other_ref, window_ref, *outs):
    me = lax.axis_index("patch")
    brick_rows = devices // 4
    brick = iota(table_ref.shape, 1)
    row = lax.rem(brick // 4 - anchor_ref[:, :1] + brick_rows, jnp.full_like(brick, brick_rows))
    place = row * 4 + brick % 4
    owner = jnp.where(brick < devices, table_ref[...], -1)
    _, rows, lanes = mine_ref.shape
    spare = iota((rows, lanes), 1) - jnp.where(iota((rows, lanes), 0) == rows - 8, SPARE, lanes)
    places = [jnp.sum(jnp.where(owner == (me ^ mask), place, 0)) for mask in masks]
    size = outs[0].shape[0]
    for s, at in enumerate(places):
        covered = at < 16
        slot = at if brick_rows <= 4 else jnp.where(covered, at, 0)
        value = (mine_ref[slot] + other_ref[slot]) * window_ref[slot]
        value = jnp.where(spare == at // 4, 2.0, value)
        value = jnp.where(spare == 4, 2.0 * (at % 4).astype(F32), value)
        if brick_rows > 4:
            value = jnp.where(covered, value, 0.0)
        outs[s // size][s % size] = value


def fill_slots(devices, masks, pieces, table, anchor, mine, other, window):
    shape = jax.ShapeDtypeStruct((len(masks) // pieces,) + mine.shape[1:], F32)
    return pl.pallas_call(
        functools.partial(slots_kernel, devices, masks),
        out_shape=[shape] * pieces,
        in_specs=[vmem()] * 5,
        out_specs=[vmem()] * pieces,
        compiler_params=params(),
        name="slots",
    )(table, anchor, mine, other, window)


def brick_kernel(side, maps, depth_curve, mine_ref, *refs):
    *others, rows_ref, cols_ref, out_ref = refs
    depth = len(depth_curve)
    wide = 2 * side
    plane = wide * wide
    tail = side * side - LANES
    per = depth * maps
    brick = mine_ref[0]
    for other in others:
        brick = brick + other[0]
    kept = 4 * per
    main, packed = brick[:kept], brick[kept:]
    rest = jnp.concatenate([packed if k == 0 else pltpu.roll(packed, LANES - tail * k, 1) for k in range(kept // 8)], axis=0)
    fill = jnp.zeros((16 - per, LANES), F32)
    mains = [jnp.concatenate([main[per * p : per * (p + 1)], fill], axis=0) for p in range(4)]
    rests = [jnp.concatenate([rest[per * p : per * (p + 1)], fill], axis=0) for p in range(4)]
    columns = []
    for d in range(-(-plane // LANES)):
        n = iota((8, LANES), 1) + d * LANES
        y = n // wide
        x = n - y * wide
        cell = (y // 2) * side + x // 2
        quarter = 2 * (y % 2) + x % 2
        lane_of = cell % LANES
        top = min((d + 1) * LANES, plane) - 1
        tiles = []
        for r in range(2):
            cut = slice(8 * r, 8 * r + 8)
            value = None
            for p in range(4):
                one = jnp.take_along_axis(mains[p][cut], lane_of, axis=1)
                if (top // wide // 2 + 1) * side > LANES:
                    one = jnp.where(cell >= LANES, jnp.take_along_axis(rests[p][cut], lane_of, axis=1), one)
                value = one if value is None else jnp.where(quarter == p, one, value)
            tiles.append(value)
        columns.append(jnp.concatenate(tiles, axis=0))
    cells = jnp.concatenate(columns, axis=1)[:, :plane]
    for z in range(depth):
        out_ref[0, pl.ds(0, maps), pl.ds(z * plane, plane)] = cells[z * maps : (z + 1) * maps]

    def noted(k):
        lane = jnp.take_along_axis(packed, jnp.full((8, LANES), SPARE + k, I32), axis=1)[0:1]
        return jnp.concatenate([lane] * (rows_ref.shape[1] // LANES), axis=1)

    counts = [noted(i) for i in range(4)]
    added = counts[0] + counts[1] + counts[2] + counts[3]
    column = noted(4)
    down = sum(counts[i] * rows_ref[pl.ds(i, 1), :] for i in range(4))
    across = sum(jnp.where(column == j * added, cols_ref[pl.ds(j, 1), :], 0.0) for j in range(4))
    window = (down * across)[:, :plane]
    for z in range(depth):
        out_ref[0, pl.ds(maps, 1), pl.ds(z * plane, plane)] = window * depth_curve[z]


def finish(side, maps, depth, mine, others):
    plane = 4 * side * side
    width = -(-plane // LANES) * LANES
    curve = bump(8 * side)
    n = np.arange(width)
    y, x = np.minimum(n // (2 * side), 2 * side - 1), n % (2 * side)
    rows = np.stack([curve[2 * side * i + y] for i in range(4)]).astype(np.float32)
    cols = np.stack([curve[2 * side * i + x] for i in range(4)]).astype(np.float32)
    depth_curve = [float(np.float32(v)) for v in bump(depth)]
    return pl.pallas_call(
        functools.partial(brick_kernel, side, maps, depth_curve),
        out_shape=jax.ShapeDtypeStruct((1, maps + 1, depth * plane), F32),
        in_specs=[vmem()] * (len(others) + 3),
        out_specs=vmem(),
        compiler_params=params(),
        name="brick",
    )(mine, *others, rows, cols)


def wire_window(side, maps, depth):
    curve_y, curve_z = bump(8 * side), bump(depth)
    cell = np.arange(side * side)
    out = np.zeros((16, 4 * depth * maps, side * side))
    for i in range(4):
        for j in range(4):
            for p in range(4):
                y = curve_y[2 * side * i + 2 * (cell // side) + p // 2]
                x = curve_y[2 * side * j + 2 * (cell % side) + p % 2]
                for z in range(depth):
                    for m in range(maps):
                        out[4 * i + j, (p * depth + z) * maps + m] = curve_z[z] * y * x
    kept = out.shape[1]
    tail = side * side - LANES
    packed = np.zeros((16, 8, LANES))
    for k in range(kept // 8):
        packed[:, :, tail * k : tail * (k + 1)] = out[:, 8 * k : 8 * k + 8, LANES:]
    return np.concatenate([out[:, :, :LANES], packed], axis=1).astype(np.float32)


def on_device(features, w_in, w_plane, w_depth, w_head, brick_owner, patch_anchor, aug_code):
    devices = lax.axis_size("patch")
    _, _, depth, cells = features.shape
    side = math.isqrt(cells) // 4
    maps = w_head.shape[0]
    levels = [1 << k for k in range(devices.bit_length() - 1)]
    paired = levels[:1] + [bit | 1 for bit in levels[1:]]
    halved = paired[1:-DIRECT]
    direct = [sum(bit for k, bit in enumerate(levels[-DIRECT:]) if q >> k & 1) | min(q, 1) for q in range(1 << DIRECT)]
    masks = [0]
    for bit in reversed(halved):
        masks = masks + [bit ^ mask for mask in masks]
    masks = [mask ^ last for mask in masks for last in direct]

    def table_round(k, table):
        return table + lax.ppermute(table, "patch", partner(devices, rounds[k]))

    rounds = paired
    table = seed_table(brick_owner, devices)
    for k in range(len(rounds)):
        table = table_round(k, table)
    plane, depth_w, head, shifted = front(aug_code, w_in, w_plane, w_depth, w_head, features[0])
    half = math.isqrt(cells)
    steps = cells // (2 * LANES)
    ready = -(-half * half // 2 // (2 * LANES)) + LEAD
    starts = [half * half * i // 4 // LANES for i in range(4)]
    span = -(-half * half // 4 // LANES)
    early = [i for i in range(4) if starts[i] + span < 2 * ready]
    late = [i for i in range(4) if i not in early]
    bricks, carry = patch_half(half, range(ready), early, starts[late[0]], False, aug_code, shifted, plane, depth_w, head)
    bricks, anchor = patch_half(
        half, range(ready, steps), late, 0, True, aug_code, shifted, plane, depth_w, head, (carry, bricks, patch_anchor)
    )
    other = lax.ppermute(bricks, "patch", partner(devices, 1))
    pieces = 2 if halved else len(direct)
    parts = fill_slots(devices, masks, pieces, table, anchor, bricks, other, wire_window(side, maps, depth))
    for k, bit in enumerate(halved):
        keep, send = parts
        got = lax.ppermute(send, "patch", partner(devices, bit))
        size = send.shape[0] // 2 if k + 1 < len(halved) else 1
        parts = [keep[i : i + size] + got[i : i + size] for i in range(0, send.shape[0], size)]
    others = [lax.ppermute(parts[q], "patch", partner(devices, direct[q])) for q in FAR_FIRST]
    return finish(side, maps, depth, parts[0], others)


def solution(mesh):
    one = P(("group", "patch"))
    in_specs = (P(("group", "patch"), None, None, None), P(), P(), P(), P(), one, one, one)
    return jax.shard_map(
        on_device, mesh=mesh, in_specs=in_specs, out_specs=P(("group", "patch"), None, None), check_vma=False
    )
```

profile of v0, /device:TPU:0, one launch (start us, length us, event | category | flops | bytes accessed | tf_op | source)
XLA Modules:
  0.0 34.4 jit_solution(5023366043605633183)
XLA Ops:
  1.3 1.9 %front.1 = (bf16[2,128,192]{2,1,0:T(8,128)(2,1)S(1)}, bf16[128,128]{1,0:T(8,128)(2,1)S(1)}, bf16[48,512]{1,0:T(8,128)(2,1)S(1)}, bf16[128,2560]{1,0:T(8,128)(2,1)S(1)}) custom-call(s32[1]{0:T(128)S(6)} %copy.16.aug_ref, bf16[28,64]{1,0:T(8,128)(2,1)} %w_in_hbm.1, bf16[9,28,28]{2,1,0:T(8,128)(2,1)} %w_plane_hbm.1, bf16[3,28,28]{2,1,0:T(8,128)(2,1)} %w_depth_hbm.1, ...), custom_call_target="tpu_custom_call" | custom-call | flops 100000000 | bytes 1048576 | tf_op jit(solution)/shard_map/front/pallas_call | solution.py:139
  3.2 2.2 %shard_map.109 = (f32[16,56,128]{2,1,0:T(8,128)S(1)}, f32[3,48,128]{2,1,0:T(8,128)S(1)}) custom-call(s32[1]{0:T(128)S(6)} %copy.16.aug_ref, bf16[128,2560]{1,0:T(8,128)(2,1)S(1)} %get-tuple-element.15.xs_ref, bf16[2,128,192]{2,1,0:T(8,128)(2,1)S(1)} %get-tuple-element.16.plane_ref, bf16[128,128]{1,0:T(8,128)(2,1)S(1)} %get-tuple-element.17.depth_ref, ...), custom_call_target="tpu_custom_call" | custom-call | flops 1000000000 | bytes 1048576 | tf_op jit(solution)/shard_map/pallas_call | solution.py:290
  5.4 0.0 copy-start
  5.4 1.4 %shard_map.110 = (f32[16,56,128]{2,1,0:T(8,128)S(1)}, s32[1,128]{1,0:T(1,128)S(1)}) custom-call(s32[1]{0:T(128)S(6)} %copy.16.aug_ref, bf16[128,2560]{1,0:T(8,128)(2,1)S(1)} %get-tuple-element.15.xs_ref, bf16[2,128,192]{2,1,0:T(8,128)(2,1)S(1)} %get-tuple-element.16.plane_ref, ...), custom_call_target="tpu_custom_call", output_to_operand_aliasing={{0}: (6, {})} | custom-call | flops 1000000000 | bytes 1048576 | tf_op jit(solution)/shard_map/pallas_call | solution.py:290
  6.9 0.0 copy-start.1
  6.9 0.0 copy-start.2
  6.9 0.6 %collective-permute-start.4 = (f32[16,56,128]{2,1,0:T(8,128)S(1)}, f32[16,56,128]{2,1,0:T(8,128)S(1)}, u32[]{:S(2)}, u32[]{:S(2)}) collective-permute-start(f32[16,56,128]{2,1,0:T(8,128)S(1)} %get-tuple-element.22.mine_ref), channel_id=1, source_target_pairs={{0,1},{1,0},{2,3},{3,2},{4,5},{5,4},{6,7},{7,6},{8,9},{9,8},{10,11... | collective-permute-start | bytes 1376264 | tf_op jit(solution)/shard_map/ppermute | solution.py:483
  8.1 0.1 collective-permute-start
  8.2 1.1 %collective-permute-done = s32[1,128]{1,0:T(1,128)S(1)} collective-permute-done((s32[1,128]{1,0:T(1,128)S(1)}, s32[1,128]{1,0:T(1,128)S(1)}, u32[]{:S(2)}, u32[]{:S(2)}) %collective-permute-start) | collective-permute-done | bytes 544 | tf_op jit(solution)/shard_map/ppermute | solution.py:465
  9.3 2.6 %collective-permute-start.1 = (s32[1,128]{1,0:T(1,128)S(1)}, s32[1,128]{1,0:T(1,128)S(1)}, u32[]{:S(2)}, u32[]{:S(2)}) collective-permute-start(s32[1,128]{1,0:T(1,128)S(1)} %add.24), channel_id=1, source_target_pairs={{0,3},{1,2},{2,1},{3,0},{4,7},{5,6},{6,5},{7,4},{8,11},{9,10},{10,... | collective-permute-start | bytes 1544 | tf_op jit(solution)/shard_map/ppermute | solution.py:465
  12.0 1.3 %collective-permute-done.1 = s32[1,128]{1,0:T(1,128)S(1)} collective-permute-done((s32[1,128]{1,0:T(1,128)S(1)}, s32[1,128]{1,0:T(1,128)S(1)}, u32[]{:S(2)}, u32[]{:S(2)}) %collective-permute-start.1) | collective-permute-done | bytes 544 | tf_op jit(solution)/shard_map/ppermute | solution.py:465
  13.3 1.8 %collective-permute-start.2 = (s32[1,128]{1,0:T(1,128)S(1)}, s32[1,128]{1,0:T(1,128)S(1)}, u32[]{:S(2)}, u32[]{:S(2)}) collective-permute-start(s32[1,128]{1,0:T(1,128)S(1)} %add.25), channel_id=1, source_target_pairs={{0,5},{1,4},{2,7},{3,6},{4,1},{5,0},{6,3},{7,2},{8,13},{9,12},{10,... | collective-permute-start | bytes 1544 | tf_op jit(solution)/shard_map/ppermute | solution.py:465
  15.0 1.3 %collective-permute-done.2 = s32[1,128]{1,0:T(1,128)S(1)} collective-permute-done((s32[1,128]{1,0:T(1,128)S(1)}, s32[1,128]{1,0:T(1,128)S(1)}, u32[]{:S(2)}, u32[]{:S(2)}) %collective-permute-start.2) | collective-permute-done | bytes 544 | tf_op jit(solution)/shard_map/ppermute | solution.py:465
  16.3 2.7 %collective-permute-start.3 = (s32[1,128]{1,0:T(1,128)S(1)}, s32[1,128]{1,0:T(1,128)S(1)}, u32[]{:S(2)}, u32[]{:S(2)}) collective-permute-start(s32[1,128]{1,0:T(1,128)S(1)} %add.26), channel_id=1, source_target_pairs={{0,9},{1,8},{2,11},{3,10},{4,13},{5,12},{6,15},{7,14},{8,1},{9,0},... | collective-permute-start | bytes 1544 | tf_op jit(solution)/shard_map/ppermute | solution.py:465
  19.0 1.3 %collective-permute-done.3 = s32[1,128]{1,0:T(1,128)S(1)} collective-permute-done((s32[1,128]{1,0:T(1,128)S(1)}, s32[1,128]{1,0:T(1,128)S(1)}, u32[]{:S(2)}, u32[]{:S(2)}) %collective-permute-start.3) | collective-permute-done | bytes 544 | tf_op jit(solution)/shard_map/ppermute | solution.py:465
  20.3 0.0 collective-permute-done.4.other_ref
  20.3 0.0 copy-done
  20.3 0.3 slots.1
  20.6 1.6 %collective-permute-start.5 = (f32[4,56,128]{2,1,0:T(8,128)S(1)}, f32[4,56,128]{2,1,0:T(8,128)S(1)}, u32[]{:S(2)}, u32[]{:S(2)}) collective-permute-start(f32[4,56,128]{2,1,0:T(8,128)S(1)} %get-tuple-element.24), channel_id=1, source_target_pairs={{0,3},{1,2},{2,1},{3,0},{4,7},{5,6},{6,5},{7,4},{8,11},{9,10},{10,... | collective-permute-start | bytes 344072 | tf_op jit(solution)/shard_map/ppermute | solution.py:488
  22.2 3.6 %collective-permute-done.5 = f32[4,56,128]{2,1,0:T(8,128)S(1)} collective-permute-done((f32[4,56,128]{2,1,0:T(8,128)S(1)}, f32[4,56,128]{2,1,0:T(8,128)S(1)}, u32[]{:S(2)}, u32[]{:S(2)}) %collective-permute-start.5) | collective-permute-done | bytes 114720 | tf_op jit(solution)/shard_map/ppermute | solution.py:488
  25.8 3.5 %collective-permute-start.6 = (f32[1,56,128]{2,1,0:T(8,128)S(1)}, f32[1,56,128]{2,1,0:T(8,128)S(1)}, u32[]{:S(2)}, u32[]{:S(2)}) collective-permute-start(f32[1,56,128]{2,1,0:T(8,128)S(1)} %get-tuple-element.27), channel_id=1, source_target_pairs={{0,13},{1,12},{2,15},{3,14},{4,9},{5,8},{6,11},{7,10},{8,5},{9,4},... | collective-permute-start | bytes 86024 | tf_op jit(solution)/shard_map/ppermute | solution.py:491
  29.3 0.0 collective-permute-start.7
  29.3 0.4 %collective-permute-start.8 = (f32[1,56,128]{2,1,0:T(8,128)S(1)}, f32[1,56,128]{2,1,0:T(8,128)S(1)}, u32[]{:S(2)}, u32[]{:S(2)}) collective-permute-start(f32[1,56,128]{2,1,0:T(8,128)S(1)} %get-tuple-element.25), channel_id=1, source_target_pairs={{0,5},{1,4},{2,7},{3,6},{4,1},{5,0},{6,3},{7,2},{8,13},{9,12},{10,... | collective-permute-start | bytes 86024 | tf_op jit(solution)/shard_map/ppermute | solution.py:491
  29.7 1.3 %collective-permute-done.6.refs_0_ = f32[1,56,128]{2,1,0:T(8,128)S(1)} collective-permute-done((f32[1,56,128]{2,1,0:T(8,128)S(1)}, f32[1,56,128]{2,1,0:T(8,128)S(1)}, u32[]{:S(2)}, u32[]{:S(2)}) %collective-permute-start.6) | collective-permute-done | bytes 28704 | tf_op jit(solution)/shard_map/ppermute | solution.py:491
  31.0 2.5 %collective-permute-done.7.refs_1_ = f32[1,56,128]{2,1,0:T(8,128)S(1)} collective-permute-done((f32[1,56,128]{2,1,0:T(8,128)S(1)}, f32[1,56,128]{2,1,0:T(8,128)S(1)}, u32[]{:S(2)}, u32[]{:S(2)}) %collective-permute-start.7) | collective-permute-done | bytes 28704 | tf_op jit(solution)/shard_map/ppermute | solution.py:491
  33.5 0.0 collective-permute-done.8.refs_2_
  33.5 0.0 copy-done.1
  33.5 0.0 copy-done.2
  33.5 0.9 %brick.1 = f32[1,4,2304]{2,1,0:T(4,128)} custom-call(f32[1,56,128]{2,1,0:T(8,128)S(1)} %get-tuple-element.28.mine_ref, f32[1,56,128]{2,1,0:T(8,128)S(1)} %collective-permute-done.6.refs_0_, f32[1,56,128]{2,1,0:T(8,128)S(1)} %collective-permute-done.7.refs_1_, f32[1,56,128]{2,1,0:T(8,128)S(1)} %collective-permute-done.8.refs_2_, f32[4,640]{1,0:T(4,128)S(1)} %copy-done.1, ...), custom_call_target="tpu_custom_call" | custom-call | tf_op jit(solution)/shard_map/brick/pallas_call | solution.py:420
  (6 shorter events, 0.0 us)
Async XLA Ops:
  5.4 14.9 %copy-start = (f32[16,56,128]{2,1,0:T(8,128)S(1)}, f32[16,56,128]{2,1,0:T(8,128)}, u32[]{:S(2)}) copy-start(f32[16,56,128]{2,1,0:T(8,128)} %constant.6.clone.window_ref) | copy-start | bytes 1376260
  6.9 26.6 %copy-start.1 = (f32[4,640]{1,0:T(4,128)S(1)}, f32[4,640]{1,0:T(4,128)}, u32[]{:S(2)}) copy-start(f32[4,640]{1,0:T(4,128)} %constant.7.clone.refs_3_) | copy-start | bytes 30724
  6.9 26.6 %copy-start.2 = (f32[4,640]{1,0:T(4,128)S(1)}, f32[4,640]{1,0:T(4,128)}, u32[]{:S(2)}) copy-start(f32[4,640]{1,0:T(4,128)} %constant.8.clone.refs_4_) | copy-start | bytes 30724
  6.9 13.4 %collective-permute-start.4 = (f32[16,56,128]{2,1,0:T(8,128)S(1)}, f32[16,56,128]{2,1,0:T(8,128)S(1)}, u32[]{:S(2)}, u32[]{:S(2)}) collective-permute-start(f32[16,56,128]{2,1,0:T(8,128)S(1)} %get-tuple-element.22.mine_ref), channel_id=1, source_target_pairs={{0,1},{1,0},{2,3},{3,2},{4,5},{5,4},{6,7},{7,6},{8,9},{9,8},{10,11... | collective-permute-start | bytes 1376264 | tf_op jit(solution)/shard_map/ppermute | solution.py:483
  8.1 1.2 %collective-permute-start = (s32[1,128]{1,0:T(1,128)S(1)}, s32[1,128]{1,0:T(1,128)S(1)}, u32[]{:S(2)}, u32[]{:S(2)}) collective-permute-start(s32[1,128]{1,0:T(1,128)S(1)} %seed.1), channel_id=1, source_target_pairs={{0,1},{1,0},{2,3},{3,2},{4,5},{5,4},{6,7},{7,6},{8,9},{9,8},{10,11... | collective-permute-start | bytes 1544 | tf_op jit(solution)/shard_map/ppermute | solution.py:465
  9.3 3.9 %collective-permute-start.1 = (s32[1,128]{1,0:T(1,128)S(1)}, s32[1,128]{1,0:T(1,128)S(1)}, u32[]{:S(2)}, u32[]{:S(2)}) collective-permute-start(s32[1,128]{1,0:T(1,128)S(1)} %add.24), channel_id=1, source_target_pairs={{0,3},{1,2},{2,1},{3,0},{4,7},{5,6},{6,5},{7,4},{8,11},{9,10},{10,... | collective-permute-start | bytes 1544 | tf_op jit(solution)/shard_map/ppermute | solution.py:465
  13.3 3.1 %collective-permute-start.2 = (s32[1,128]{1,0:T(1,128)S(1)}, s32[1,128]{1,0:T(1,128)S(1)}, u32[]{:S(2)}, u32[]{:S(2)}) collective-permute-start(s32[1,128]{1,0:T(1,128)S(1)} %add.25), channel_id=1, source_target_pairs={{0,5},{1,4},{2,7},{3,6},{4,1},{5,0},{6,3},{7,2},{8,13},{9,12},{10,... | collective-permute-start | bytes 1544 | tf_op jit(solution)/shard_map/ppermute | solution.py:465
  16.3 4.0 %collective-permute-start.3 = (s32[1,128]{1,0:T(1,128)S(1)}, s32[1,128]{1,0:T(1,128)S(1)}, u32[]{:S(2)}, u32[]{:S(2)}) collective-permute-start(s32[1,128]{1,0:T(1,128)S(1)} %add.26), channel_id=1, source_target_pairs={{0,9},{1,8},{2,11},{3,10},{4,13},{5,12},{6,15},{7,14},{8,1},{9,0},... | collective-permute-start | bytes 1544 | tf_op jit(solution)/shard_map/ppermute | solution.py:465
  20.6 5.2 %collective-permute-start.5 = (f32[4,56,128]{2,1,0:T(8,128)S(1)}, f32[4,56,128]{2,1,0:T(8,128)S(1)}, u32[]{:S(2)}, u32[]{:S(2)}) collective-permute-start(f32[4,56,128]{2,1,0:T(8,128)S(1)} %get-tuple-element.24), channel_id=1, source_target_pairs={{0,3},{1,2},{2,1},{3,0},{4,7},{5,6},{6,5},{7,4},{8,11},{9,10},{10,... | collective-permute-start | bytes 344072 | tf_op jit(solution)/shard_map/ppermute | solution.py:488
  25.8 5.2 %collective-permute-start.6 = (f32[1,56,128]{2,1,0:T(8,128)S(1)}, f32[1,56,128]{2,1,0:T(8,128)S(1)}, u32[]{:S(2)}, u32[]{:S(2)}) collective-permute-start(f32[1,56,128]{2,1,0:T(8,128)S(1)} %get-tuple-element.27), channel_id=1, source_target_pairs={{0,13},{1,12},{2,15},{3,14},{4,9},{5,8},{6,11},{7,10},{8,5},{9,4},... | collective-permute-start | bytes 86024 | tf_op jit(solution)/shard_map/ppermute | solution.py:491
  29.3 4.2 %collective-permute-start.7 = (f32[1,56,128]{2,1,0:T(8,128)S(1)}, f32[1,56,128]{2,1,0:T(8,128)S(1)}, u32[]{:S(2)}, u32[]{:S(2)}) collective-permute-start(f32[1,56,128]{2,1,0:T(8,128)S(1)} %get-tuple-element.26), channel_id=1, source_target_pairs={{0,9},{1,8},{2,11},{3,10},{4,13},{5,12},{6,15},{7,14},{8,1},{9,0},... | collective-permute-start | bytes 86024 | tf_op jit(solution)/shard_map/ppermute | solution.py:491
  29.3 4.2 %collective-permute-start.8 = (f32[1,56,128]{2,1,0:T(8,128)S(1)}, f32[1,56,128]{2,1,0:T(8,128)S(1)}, u32[]{:S(2)}, u32[]{:S(2)}) collective-permute-start(f32[1,56,128]{2,1,0:T(8,128)S(1)} %get-tuple-element.25), channel_id=1, source_target_pairs={{0,5},{1,4},{2,7},{3,6},{4,1},{5,0},{6,3},{7,2},{8,13},{9,12},{10,... | collective-permute-start | bytes 86024 | tf_op jit(solution)/shard_map/ppermute | solution.py:491
where the time goes:
time: 34.5 us; the launch traced here: 34.4 us
  starting transfers between devices  13.2 us (38%)
  waiting for transfers between devices  12.4 us (36%)
  Pallas kernels  6.69 us (19%)
  between operations  2.03 us (6%)
    ppermute x4, starting transfers between devices, table_round(): return table + lax.ppermute(table, 'patch', partner(devices, rounds[k]))  7.17 us
    ppermute x4, waiting for transfers between devices, table_round(): return table + lax.ppermute(table, 'patch', partner(devices, rounds[k]))  5.03 us
    ppermute x3, starting transfers between devices, on_device(): lax.ppermute(parts[q], 'patch', partner(devices, direct[q]))  3.9 us
    ppermute x3, waiting for transfers between devices, on_device(): lax.ppermute(parts[q], 'patch', partner(devices, direct[q]))  3.75 us
    pallas_call x2, Pallas kernels, patch_half(): pl.pallas_call(functools.partial(patch_kernel, half, tiles, brick_rows, k...  3.66 us
    ppermute x1, waiting for transfers between devices, on_device(): got = lax.ppermute(send, 'patch', partner(devices, bit))  3.61 us
    pallas_call x1, Pallas kernels, front(): pl.pallas_call(front_kernel, out_shape=[jax.ShapeDtypeStruct(s, BF16) for...  1.87 us
    ppermute x1, starting transfers between devices, on_device(): got = lax.ppermute(send, 'patch', partner(devices, bit))  1.6 us
  transfers between devices with their start and end apart: 9, of which 7 were waited for; matrix products, arithmetic and copies ran while one was open for 0% of the time, Pallas kernels for 0%

commit v1 on v0

--- a/solution.py
+++ b/solution.py
@@ -461,13 +461,14 @@
         masks = masks + [bit ^ mask for mask in masks]
     masks = [mask ^ last for mask in masks for last in direct]
 
-    def table_round(k, table):
-        return table + lax.ppermute(table, "patch", partner(devices, rounds[k]))
-
-    rounds = paired
     table = seed_table(brick_owner, devices)
-    for k in range(len(rounds)):
-        table = table_round(k, table)
+    for bit in halved:
+        table = table + lax.ppermute(table, "patch", partner(devices, bit))
+    reached = []
+    for q in FAR_FIRST:
+        reached.append(lax.ppermute(table, "patch", partner(devices, direct[q])))
+    table = functools.reduce(lambda a, b: a + b, reached, table)
+    table = table + lax.ppermute(table, "patch", partner(devices, 1))
     plane, depth_w, head, shifted = front(aug_code, w_in, w_plane, w_depth, w_head, features[0])
     half = math.isqrt(cells)
     steps = cells // (2 * LANES)

time: 34.5 us -> 34.1 us (0.988)
  starting transfers between devices: 13.2 us -> 12.6 us
    ppermute x3, waiting for transfers between devices: 3.75 us -> 2.62 us  [on_device(): lax.ppermute(parts[q], 'patch', partner(devices, direct[q]))]
    ppermute x4 -> x5, waiting for transfers between devices: 5.03 us -> 6.16 us  [the longest x3 3.71 us: on_device(): reached.append(lax.ppermute(table, 'patch', partner(devices, direct[q])))]
    ppermute x4 -> x5, starting transfers between devices: 7.17 us -> 6.72 us  [the longest x3 3.96 us: on_device(): reached.append(lax.ppermute(table, 'patch', partner(devices, direct[q])))]
  transfers between devices with their start and end apart: 9 -> 10, of which waited for: 7 -> 7; matrix products, arithmetic and copies ran while one was open for 0% -> 0% of each run, Pallas kernels for 0% -> 0%
where the time goes in v1:
time: 34.1 us; the launch traced here: 33.9 us
  starting transfers between devices  12.6 us (37%)
  waiting for transfers between devices  12.6 us (37%)
  Pallas kernels  6.69 us (20%)
  between operations  2.03 us (6%)
    ppermute x3, starting transfers between devices, on_device(): reached.append(lax.ppermute(table, 'patch', partner(devices, direct[q])))  3.96 us
    ppermute x3, starting transfers between devices, on_device(): lax.ppermute(parts[q], 'patch', partner(devices, direct[q]))  3.95 us
    ppermute x1, waiting for transfers between devices, on_device(): got = lax.ppermute(send, 'patch', partner(devices, bit))  3.8 us
    ppermute x3, waiting for transfers between devices, on_device(): reached.append(lax.ppermute(table, 'patch', partner(devices, direct[q])))  3.71 us
    pallas_call x2, Pallas kernels, patch_half(): pl.pallas_call(functools.partial(patch_kernel, half, tiles, brick_rows, k...  3.66 us
    ppermute x1, starting transfers between devices, on_device(): table = table + lax.ppermute(table, 'patch', partner(devices, bit))  2.68 us
    ppermute x3, waiting for transfers between devices, on_device(): lax.ppermute(parts[q], 'patch', partner(devices, direct[q]))  2.62 us
    pallas_call x1, Pallas kernels, front(): pl.pallas_call(front_kernel, out_shape=[jax.ShapeDtypeStruct(s, BF16) for...  1.87 us
  transfers between devices with their start and end apart: 10, of which 7 were waited for; matrix products, arithmetic and copies ran while one was open for 0% of the time, Pallas kernels for 0%

profile of v1, /device:TPU:0, one launch (start us, length us, event | category | flops | bytes accessed | tf_op | source)
XLA Modules:
  0.0 33.9 jit_solution(12663620835677472989)
XLA Ops:
  1.3 1.9 %front.1 = (bf16[2,128,192]{2,1,0:T(8,128)(2,1)S(1)}, bf16[128,128]{1,0:T(8,128)(2,1)S(1)}, bf16[48,512]{1,0:T(8,128)(2,1)S(1)}, bf16[128,2560]{1,0:T(8,128)(2,1)S(1)}) custom-call(s32[1]{0:T(128)S(6)} %copy.16.aug_ref, bf16[28,64]{1,0:T(8,128)(2,1)} %w_in_hbm.1, bf16[9,28,28]{2,1,0:T(8,128)(2,1)} %w_plane_hbm.1, bf16[3,28,28]{2,1,0:T(8,128)(2,1)} %w_depth_hbm.1, ...), custom_call_target="tpu_custom_call" | custom-call | flops 100000000 | bytes 1048576 | tf_op jit(solution)/shard_map/front/pallas_call | solution.py:139
  3.2 2.2 %shard_map.109 = (f32[16,56,128]{2,1,0:T(8,128)S(1)}, f32[3,48,128]{2,1,0:T(8,128)S(1)}) custom-call(s32[1]{0:T(128)S(6)} %copy.16.aug_ref, bf16[128,2560]{1,0:T(8,128)(2,1)S(1)} %get-tuple-element.15.xs_ref, bf16[2,128,192]{2,1,0:T(8,128)(2,1)S(1)} %get-tuple-element.16.plane_ref, bf16[128,128]{1,0:T(8,128)(2,1)S(1)} %get-tuple-element.17.depth_ref, ...), custom_call_target="tpu_custom_call" | custom-call | flops 1000000000 | bytes 1048576 | tf_op jit(solution)/shard_map/pallas_call | solution.py:290
  5.4 0.0 copy-start
  5.4 1.4 %shard_map.110 = (f32[16,56,128]{2,1,0:T(8,128)S(1)}, s32[1,128]{1,0:T(1,128)S(1)}) custom-call(s32[1]{0:T(128)S(6)} %copy.16.aug_ref, bf16[128,2560]{1,0:T(8,128)(2,1)S(1)} %get-tuple-element.15.xs_ref, bf16[2,128,192]{2,1,0:T(8,128)(2,1)S(1)} %get-tuple-element.16.plane_ref, ...), custom_call_target="tpu_custom_call", output_to_operand_aliasing={{0}: (6, {})} | custom-call | flops 1000000000 | bytes 1048576 | tf_op jit(solution)/shard_map/pallas_call | solution.py:290
  6.9 0.0 copy-start.1
  6.9 0.0 copy-start.2
  6.9 0.6 %collective-permute-start.5 = (f32[16,56,128]{2,1,0:T(8,128)S(1)}, f32[16,56,128]{2,1,0:T(8,128)S(1)}, u32[]{:S(2)}, u32[]{:S(2)}) collective-permute-start(f32[16,56,128]{2,1,0:T(8,128)S(1)} %get-tuple-element.22.mine_ref), channel_id=1, source_target_pairs={{0,1},{1,0},{2,3},{3,2},{4,5},{5,4},{6,7},{7,6},{8,9},{9,8},{10,11... | collective-permute-start | bytes 1376264 | tf_op jit(solution)/shard_map/ppermute | solution.py:484
  8.1 2.7 %collective-permute-start = (s32[1,128]{1,0:T(1,128)S(1)}, s32[1,128]{1,0:T(1,128)S(1)}, u32[]{:S(2)}, u32[]{:S(2)}) collective-permute-start(s32[1,128]{1,0:T(1,128)S(1)} %seed.1), channel_id=1, source_target_pairs={{0,3},{1,2},{2,1},{3,0},{4,7},{5,6},{6,5},{7,4},{8,11},{9,10},{10,... | collective-permute-start | bytes 1544 | tf_op jit(solution)/shard_map/ppermute | solution.py:466
  10.8 1.3 %collective-permute-done = s32[1,128]{1,0:T(1,128)S(1)} collective-permute-done((s32[1,128]{1,0:T(1,128)S(1)}, s32[1,128]{1,0:T(1,128)S(1)}, u32[]{:S(2)}, u32[]{:S(2)}) %collective-permute-start) | collective-permute-done | bytes 544 | tf_op jit(solution)/shard_map/ppermute | solution.py:466
  12.1 3.8 %collective-permute-start.1 = (s32[1,128]{1,0:T(1,128)S(1)}, s32[1,128]{1,0:T(1,128)S(1)}, u32[]{:S(2)}, u32[]{:S(2)}) collective-permute-start(s32[1,128]{1,0:T(1,128)S(1)} %add.27), channel_id=1, source_target_pairs={{0,13},{1,12},{2,15},{3,14},{4,9},{5,8},{6,11},{7,10},{8,5},{9,4},... | collective-permute-start | bytes 1544 | tf_op jit(solution)/shard_map/ppermute | solution.py:469
  15.9 0.0 collective-permute-start.2
  15.9 0.2 collective-permute-start.3
  16.1 1.1 %collective-permute-done.1 = s32[1,128]{1,0:T(1,128)S(1)} collective-permute-done((s32[1,128]{1,0:T(1,128)S(1)}, s32[1,128]{1,0:T(1,128)S(1)}, u32[]{:S(2)}, u32[]{:S(2)}) %collective-permute-start.1) | collective-permute-done | bytes 544 | tf_op jit(solution)/shard_map/ppermute | solution.py:469
  17.2 2.6 %collective-permute-done.2 = s32[1,128]{1,0:T(1,128)S(1)} collective-permute-done((s32[1,128]{1,0:T(1,128)S(1)}, s32[1,128]{1,0:T(1,128)S(1)}, u32[]{:S(2)}, u32[]{:S(2)}) %collective-permute-start.2) | collective-permute-done | bytes 544 | tf_op jit(solution)/shard_map/ppermute | solution.py:469
  19.8 0.0 collective-permute-done.3
  19.8 0.1 collective-permute-start.4
  19.9 1.1 %collective-permute-done.4 = s32[1,128]{1,0:T(1,128)S(1)} collective-permute-done((s32[1,128]{1,0:T(1,128)S(1)}, s32[1,128]{1,0:T(1,128)S(1)}, u32[]{:S(2)}, u32[]{:S(2)}) %collective-permute-start.4) | collective-permute-done | bytes 544 | tf_op jit(solution)/shard_map/ppermute | solution.py:471
  21.0 0.0 collective-permute-done.5.other_ref
  21.0 0.0 copy-done
  21.0 0.3 slots.1
  21.3 1.4 %collective-permute-start.6 = (f32[4,56,128]{2,1,0:T(8,128)S(1)}, f32[4,56,128]{2,1,0:T(8,128)S(1)}, u32[]{:S(2)}, u32[]{:S(2)}) collective-permute-start(f32[4,56,128]{2,1,0:T(8,128)S(1)} %get-tuple-element.24), channel_id=1, source_target_pairs={{0,3},{1,2},{2,1},{3,0},{4,7},{5,6},{6,5},{7,4},{8,11},{9,10},{10,... | collective-permute-start | bytes 344072 | tf_op jit(solution)/shard_map/ppermute | solution.py:489
  22.7 3.8 %collective-permute-done.6 = f32[4,56,128]{2,1,0:T(8,128)S(1)} collective-permute-done((f32[4,56,128]{2,1,0:T(8,128)S(1)}, f32[4,56,128]{2,1,0:T(8,128)S(1)}, u32[]{:S(2)}, u32[]{:S(2)}) %collective-permute-start.6) | collective-permute-done | bytes 114720 | tf_op jit(solution)/shard_map/ppermute | solution.py:489
  26.5 1.3 %collective-permute-start.7 = (f32[1,56,128]{2,1,0:T(8,128)S(1)}, f32[1,56,128]{2,1,0:T(8,128)S(1)}, u32[]{:S(2)}, u32[]{:S(2)}) collective-permute-start(f32[1,56,128]{2,1,0:T(8,128)S(1)} %get-tuple-element.27), channel_id=1, source_target_pairs={{0,13},{1,12},{2,15},{3,14},{4,9},{5,8},{6,11},{7,10},{8,5},{9,4},... | collective-permute-start | bytes 86024 | tf_op jit(solution)/shard_map/ppermute | solution.py:492
  27.8 0.4 %collective-permute-start.8 = (f32[1,56,128]{2,1,0:T(8,128)S(1)}, f32[1,56,128]{2,1,0:T(8,128)S(1)}, u32[]{:S(2)}, u32[]{:S(2)}) collective-permute-start(f32[1,56,128]{2,1,0:T(8,128)S(1)} %get-tuple-element.26), channel_id=1, source_target_pairs={{0,9},{1,8},{2,11},{3,10},{4,13},{5,12},{6,15},{7,14},{8,1},{9,0},... | collective-permute-start | bytes 86024 | tf_op jit(solution)/shard_map/ppermute | solution.py:492
  28.1 2.3 %collective-permute-start.9 = (f32[1,56,128]{2,1,0:T(8,128)S(1)}, f32[1,56,128]{2,1,0:T(8,128)S(1)}, u32[]{:S(2)}, u32[]{:S(2)}) collective-permute-start(f32[1,56,128]{2,1,0:T(8,128)S(1)} %get-tuple-element.25), channel_id=1, source_target_pairs={{0,5},{1,4},{2,7},{3,6},{4,1},{5,0},{6,3},{7,2},{8,13},{9,12},{10,... | collective-permute-start | bytes 86024 | tf_op jit(solution)/shard_map/ppermute | solution.py:492
  30.4 1.2 %collective-permute-done.7.refs_0_ = f32[1,56,128]{2,1,0:T(8,128)S(1)} collective-permute-done((f32[1,56,128]{2,1,0:T(8,128)S(1)}, f32[1,56,128]{2,1,0:T(8,128)S(1)}, u32[]{:S(2)}, u32[]{:S(2)}) %collective-permute-start.7) | collective-permute-done | bytes 28704 | tf_op jit(solution)/shard_map/ppermute | solution.py:492
  31.6 1.4 %collective-permute-done.8.refs_1_ = f32[1,56,128]{2,1,0:T(8,128)S(1)} collective-permute-done((f32[1,56,128]{2,1,0:T(8,128)S(1)}, f32[1,56,128]{2,1,0:T(8,128)S(1)}, u32[]{:S(2)}, u32[]{:S(2)}) %collective-permute-start.8) | collective-permute-done | bytes 28704 | tf_op jit(solution)/shard_map/ppermute | solution.py:492
  33.1 0.0 collective-permute-done.9.refs_2_
  33.1 0.0 copy-done.1
  33.1 0.0 copy-done.2
  33.1 0.9 %brick.1 = f32[1,4,2304]{2,1,0:T(4,128)} custom-call(f32[1,56,128]{2,1,0:T(8,128)S(1)} %get-tuple-element.28.mine_ref, f32[1,56,128]{2,1,0:T(8,128)S(1)} %collective-permute-done.7.refs_0_, f32[1,56,128]{2,1,0:T(8,128)S(1)} %collective-permute-done.8.refs_1_, f32[1,56,128]{2,1,0:T(8,128)S(1)} %collective-permute-done.9.refs_2_, f32[4,640]{1,0:T(4,128)S(1)} %copy-done.1, ...), custom_call_target="tpu_custom_call" | custom-call | tf_op jit(solution)/shard_map/brick/pallas_call | solution.py:420
  (5 shorter events, 0.0 us)
Async XLA Ops:
  5.4 15.6 %copy-start = (f32[16,56,128]{2,1,0:T(8,128)S(1)}, f32[16,56,128]{2,1,0:T(8,128)}, u32[]{:S(2)}) copy-start(f32[16,56,128]{2,1,0:T(8,128)} %constant.6.clone.window_ref) | copy-start | bytes 1376260
  6.9 26.2 %copy-start.1 = (f32[4,640]{1,0:T(4,128)S(1)}, f32[4,640]{1,0:T(4,128)}, u32[]{:S(2)}) copy-start(f32[4,640]{1,0:T(4,128)} %constant.7.clone.refs_3_) | copy-start | bytes 30724
  6.9 26.2 %copy-start.2 = (f32[4,640]{1,0:T(4,128)S(1)}, f32[4,640]{1,0:T(4,128)}, u32[]{:S(2)}) copy-start(f32[4,640]{1,0:T(4,128)} %constant.8.clone.refs_4_) | copy-start | bytes 30724
  6.9 14.1 %collective-permute-start.5 = (f32[16,56,128]{2,1,0:T(8,128)S(1)}, f32[16,56,128]{2,1,0:T(8,128)S(1)}, u32[]{:S(2)}, u32[]{:S(2)}) collective-permute-start(f32[16,56,128]{2,1,0:T(8,128)S(1)} %get-tuple-element.22.mine_ref), channel_id=1, source_target_pairs={{0,1},{1,0},{2,3},{3,2},{4,5},{5,4},{6,7},{7,6},{8,9},{9,8},{10,11... | collective-permute-start | bytes 1376264 | tf_op jit(solution)/shard_map/ppermute | solution.py:484
  8.1 4.0 %collective-permute-start = (s32[1,128]{1,0:T(1,128)S(1)}, s32[1,128]{1,0:T(1,128)S(1)}, u32[]{:S(2)}, u32[]{:S(2)}) collective-permute-start(s32[1,128]{1,0:T(1,128)S(1)} %seed.1), channel_id=1, source_target_pairs={{0,3},{1,2},{2,1},{3,0},{4,7},{5,6},{6,5},{7,4},{8,11},{9,10},{10,... | collective-permute-start | bytes 1544 | tf_op jit(solution)/shard_map/ppermute | solution.py:466
  12.1 5.1 %collective-permute-start.1 = (s32[1,128]{1,0:T(1,128)S(1)}, s32[1,128]{1,0:T(1,128)S(1)}, u32[]{:S(2)}, u32[]{:S(2)}) collective-permute-start(s32[1,128]{1,0:T(1,128)S(1)} %add.27), channel_id=1, source_target_pairs={{0,13},{1,12},{2,15},{3,14},{4,9},{5,8},{6,11},{7,10},{8,5},{9,4},... | collective-permute-start | bytes 1544 | tf_op jit(solution)/shard_map/ppermute | solution.py:469
  15.9 3.9 %collective-permute-start.2 = (s32[1,128]{1,0:T(1,128)S(1)}, s32[1,128]{1,0:T(1,128)S(1)}, u32[]{:S(2)}, u32[]{:S(2)}) collective-permute-start(s32[1,128]{1,0:T(1,128)S(1)} %add.27), channel_id=1, source_target_pairs={{0,9},{1,8},{2,11},{3,10},{4,13},{5,12},{6,15},{7,14},{8,1},{9,0},... | collective-permute-start | bytes 1544 | tf_op jit(solution)/shard_map/ppermute | solution.py:469
  15.9 3.9 %collective-permute-start.3 = (s32[1,128]{1,0:T(1,128)S(1)}, s32[1,128]{1,0:T(1,128)S(1)}, u32[]{:S(2)}, u32[]{:S(2)}) collective-permute-start(s32[1,128]{1,0:T(1,128)S(1)} %add.27), channel_id=1, source_target_pairs={{0,5},{1,4},{2,7},{3,6},{4,1},{5,0},{6,3},{7,2},{8,13},{9,12},{10,... | collective-permute-start | bytes 1544 | tf_op jit(solution)/shard_map/ppermute | solution.py:469
  19.8 1.2 %collective-permute-start.4 = (s32[1,128]{1,0:T(1,128)S(1)}, s32[1,128]{1,0:T(1,128)S(1)}, u32[]{:S(2)}, u32[]{:S(2)}) collective-permute-start(s32[1,128]{1,0:T(1,128)S(1)} %add_add_fusion), channel_id=1, source_target_pairs={{0,1},{1,0},{2,3},{3,2},{4,5},{5,4},{6,7},{7,6},{8,9},{9,8},{10,11... | collective-permute-start | bytes 1544 | tf_op jit(solution)/shard_map/ppermute | solution.py:471
  21.3 5.2 %collective-permute-start.6 = (f32[4,56,128]{2,1,0:T(8,128)S(1)}, f32[4,56,128]{2,1,0:T(8,128)S(1)}, u32[]{:S(2)}, u32[]{:S(2)}) collective-permute-start(f32[4,56,128]{2,1,0:T(8,128)S(1)} %get-tuple-element.24), channel_id=1, source_target_pairs={{0,3},{1,2},{2,1},{3,0},{4,7},{5,6},{6,5},{7,4},{8,11},{9,10},{10,... | collective-permute-start | bytes 344072 | tf_op jit(solution)/shard_map/ppermute | solution.py:489
  26.5 5.2 %collective-permute-start.7 = (f32[1,56,128]{2,1,0:T(8,128)S(1)}, f32[1,56,128]{2,1,0:T(8,128)S(1)}, u32[]{:S(2)}, u32[]{:S(2)}) collective-permute-start(f32[1,56,128]{2,1,0:T(8,128)S(1)} %get-tuple-element.27), channel_id=1, source_target_pairs={{0,13},{1,12},{2,15},{3,14},{4,9},{5,8},{6,11},{7,10},{8,5},{9,4},... | collective-permute-start | bytes 86024 | tf_op jit(solution)/shard_map/ppermute | solution.py:492
  27.8 5.3 %collective-permute-start.8 = (f32[1,56,128]{2,1,0:T(8,128)S(1)}, f32[1,56,128]{2,1,0:T(8,128)S(1)}, u32[]{:S(2)}, u32[]{:S(2)}) collective-permute-start(f32[1,56,128]{2,1,0:T(8,128)S(1)} %get-tuple-element.26), channel_id=1, source_target_pairs={{0,9},{1,8},{2,11},{3,10},{4,13},{5,12},{6,15},{7,14},{8,1},{9,0},... | collective-permute-start | bytes 86024 | tf_op jit(solution)/shard_map/ppermute | solution.py:492
  28.1 4.9 %collective-permute-start.9 = (f32[1,56,128]{2,1,0:T(8,128)S(1)}, f32[1,56,128]{2,1,0:T(8,128)S(1)}, u32[]{:S(2)}, u32[]{:S(2)}) collective-permute-start(f32[1,56,128]{2,1,0:T(8,128)S(1)} %get-tuple-element.25), channel_id=1, source_target_pairs={{0,5},{1,4},{2,7},{3,6},{4,1},{5,0},{6,3},{7,2},{8,13},{9,12},{10,... | collective-permute-start | bytes 86024 | tf_op jit(solution)/shard_map/ppermute | solution.py:492

commit v2 on v0

--- a/solution.py
+++ b/solution.py
@@ -454,12 +454,12 @@
     maps = w_head.shape[0]
     levels = [1 << k for k in range(devices.bit_length() - 1)]
     paired = levels[:1] + [bit | 1 for bit in levels[1:]]
-    halved = paired[1:-DIRECT]
-    direct = [sum(bit for k, bit in enumerate(levels[-DIRECT:]) if q >> k & 1) | min(q, 1) for q in range(1 << DIRECT)]
+    halved = paired[1 + DIRECT :]
+    direct = [sum(bit for k, bit in enumerate(levels[1 : 1 + DIRECT]) if q >> k & 1) | min(q, 1) for q in range(1 << DIRECT)]
     masks = [0]
     for bit in reversed(halved):
         masks = masks + [bit ^ mask for mask in masks]
-    masks = [mask ^ last for mask in masks for last in direct]
+    masks = [first ^ mask for first in direct for mask in masks]
 
     def table_round(k, table):
         return table + lax.ppermute(table, "patch", partner(devices, rounds[k]))
@@ -481,15 +481,13 @@
         half, range(ready, steps), late, 0, True, aug_code, shifted, plane, depth_w, head, (carry, bricks, patch_anchor)
     )
     other = lax.ppermute(bricks, "patch", partner(devices, 1))
-    pieces = 2 if halved else len(direct)
-    parts = fill_slots(devices, masks, pieces, table, anchor, bricks, other, wire_window(side, maps, depth))
-    for k, bit in enumerate(halved):
-        keep, send = parts
-        got = lax.ppermute(send, "patch", partner(devices, bit))
-        size = send.shape[0] // 2 if k + 1 < len(halved) else 1
-        parts = [keep[i : i + size] + got[i : i + size] for i in range(0, send.shape[0], size)]
-    others = [lax.ppermute(parts[q], "patch", partner(devices, direct[q])) for q in FAR_FIRST]
-    return finish(side, maps, depth, parts[0], others)
+    parts = fill_slots(devices, masks, len(direct), table, anchor, bricks, other, wire_window(side, maps, depth))
+    sums = [parts[0]] + [lax.ppermute(parts[q], "patch", partner(devices, direct[q])) for q in FAR_FIRST]
+    for bit in halved:
+        size = sums[0].shape[0] // 2
+        keep, send = (functools.reduce(lambda a, b: a + b, [one[k : k + size] for one in sums]) for k in (0, size))
+        sums = [keep, lax.ppermute(send, "patch", partner(devices, bit))]
+    return finish(side, maps, depth, sums[0], sums[1:])
 
 
 def solution(mesh):

time: 34.5 us -> 32.5 us (0.942)
  waiting for transfers between devices: 12.4 us -> 10.2 us
    ppermute x1, waiting for transfers between devices: 3.61 us -> 1.65 us  [on_device(): sums = [keep, lax.ppermute(send, 'patch', partner(devices, bit))]]
    ppermute x1, starting transfers between devices: 1.6 us -> 2.61 us  [on_device(): sums = [keep, lax.ppermute(send, 'patch', partner(devices, bit))]]
    ppermute x3, starting transfers between devices: 3.9 us -> 3.02 us  [on_device(): lax.ppermute(parts[q], 'patch', partner(devices, direct[q]))]
  transfers between devices with their start and end apart: 9 -> 9, of which waited for: 7 -> 8; matrix products, arithmetic and copies ran while one was open for 0% -> 0% of each run, Pallas kernels for 0% -> 0%
where the time goes in v2:
time: 32.5 us; the launch traced here: 32.3 us
  starting transfers between devices  13.4 us (41%)
  waiting for transfers between devices  10.2 us (31%)
  Pallas kernels  6.69 us (21%)
  between operations  2.03 us (6%)
    ppermute x4, starting transfers between devices, table_round(): return table + lax.ppermute(table, 'patch', partner(devices, rounds[k]))  7.17 us
    ppermute x4, waiting for transfers between devices, table_round(): return table + lax.ppermute(table, 'patch', partner(devices, rounds[k]))  5.03 us
    pallas_call x2, Pallas kernels, patch_half(): pl.pallas_call(functools.partial(patch_kernel, half, tiles, brick_rows, k...  3.66 us
    ppermute x3, waiting for transfers between devices, on_device(): lax.ppermute(parts[q], 'patch', partner(devices, direct[q]))  3.5 us
    ppermute x3, starting transfers between devices, on_device(): lax.ppermute(parts[q], 'patch', partner(devices, direct[q]))  3.02 us
    ppermute x1, starting transfers between devices, on_device(): sums = [keep, lax.ppermute(send, 'patch', partner(devices, bit))]  2.61 us
    pallas_call x1, Pallas kernels, front(): pl.pallas_call(front_kernel, out_shape=[jax.ShapeDtypeStruct(s, BF16) for...  1.87 us
    ppermute x1, waiting for transfers between devices, on_device(): sums = [keep, lax.ppermute(send, 'patch', partner(devices, bit))]  1.65 us
  transfers between devices with their start and end apart: 9, of which 8 were waited for; matrix products, arithmetic and copies ran while one was open for 0% of the time, Pallas kernels for 0%

profile of v2, /device:TPU:0, one launch (start us, length us, event | category | flops | bytes accessed | tf_op | source)
XLA Modules:
  0.0 32.3 jit_solution(14884697199380451460)
XLA Ops:
  1.3 1.9 %front.1 = (bf16[2,128,192]{2,1,0:T(8,128)(2,1)S(1)}, bf16[128,128]{1,0:T(8,128)(2,1)S(1)}, bf16[48,512]{1,0:T(8,128)(2,1)S(1)}, bf16[128,2560]{1,0:T(8,128)(2,1)S(1)}) custom-call(s32[1]{0:T(128)S(6)} %copy.16.aug_ref, bf16[28,64]{1,0:T(8,128)(2,1)} %w_in_hbm.1, bf16[9,28,28]{2,1,0:T(8,128)(2,1)} %w_plane_hbm.1, bf16[3,28,28]{2,1,0:T(8,128)(2,1)} %w_depth_hbm.1, ...), custom_call_target="tpu_custom_call" | custom-call | flops 100000000 | bytes 1048576 | tf_op jit(solution)/shard_map/front/pallas_call | solution.py:139
  3.2 2.2 %shard_map.109 = (f32[16,56,128]{2,1,0:T(8,128)S(1)}, f32[3,48,128]{2,1,0:T(8,128)S(1)}) custom-call(s32[1]{0:T(128)S(6)} %copy.16.aug_ref, bf16[128,2560]{1,0:T(8,128)(2,1)S(1)} %get-tuple-element.17.xs_ref, bf16[2,128,192]{2,1,0:T(8,128)(2,1)S(1)} %get-tuple-element.18.plane_ref, bf16[128,128]{1,0:T(8,128)(2,1)S(1)} %get-tuple-element.19.depth_ref, ...), custom_call_target="tpu_custom_call" | custom-call | flops 1000000000 | bytes 1048576 | tf_op jit(solution)/shard_map/pallas_call | solution.py:290
  5.4 0.0 copy-start
  5.4 1.4 %shard_map.110 = (f32[16,56,128]{2,1,0:T(8,128)S(1)}, s32[1,128]{1,0:T(1,128)S(1)}) custom-call(s32[1]{0:T(128)S(6)} %copy.16.aug_ref, bf16[128,2560]{1,0:T(8,128)(2,1)S(1)} %get-tuple-element.17.xs_ref, bf16[2,128,192]{2,1,0:T(8,128)(2,1)S(1)} %get-tuple-element.18.plane_ref, ...), custom_call_target="tpu_custom_call", output_to_operand_aliasing={{0}: (6, {})} | custom-call | flops 1000000000 | bytes 1048576 | tf_op jit(solution)/shard_map/pallas_call | solution.py:290
  6.9 0.0 copy-start.1
  6.9 0.0 copy-start.2
  6.9 0.6 %collective-permute-start.4 = (f32[16,56,128]{2,1,0:T(8,128)S(1)}, f32[16,56,128]{2,1,0:T(8,128)S(1)}, u32[]{:S(2)}, u32[]{:S(2)}) collective-permute-start(f32[16,56,128]{2,1,0:T(8,128)S(1)} %get-tuple-element.24.mine_ref), channel_id=1, source_target_pairs={{0,1},{1,0},{2,3},{3,2},{4,5},{5,4},{6,7},{7,6},{8,9},{9,8},{10,11... | collective-permute-start | bytes 1376264 | tf_op jit(solution)/shard_map/ppermute | solution.py:483
  8.1 0.1 collective-permute-start
  8.2 1.1 %collective-permute-done = s32[1,128]{1,0:T(1,128)S(1)} collective-permute-done((s32[1,128]{1,0:T(1,128)S(1)}, s32[1,128]{1,0:T(1,128)S(1)}, u32[]{:S(2)}, u32[]{:S(2)}) %collective-permute-start) | collective-permute-done | bytes 544 | tf_op jit(solution)/shard_map/ppermute | solution.py:465
  9.3 2.6 %collective-permute-start.1 = (s32[1,128]{1,0:T(1,128)S(1)}, s32[1,128]{1,0:T(1,128)S(1)}, u32[]{:S(2)}, u32[]{:S(2)}) collective-permute-start(s32[1,128]{1,0:T(1,128)S(1)} %add.30), channel_id=1, source_target_pairs={{0,3},{1,2},{2,1},{3,0},{4,7},{5,6},{6,5},{7,4},{8,11},{9,10},{10,... | collective-permute-start | bytes 1544 | tf_op jit(solution)/shard_map/ppermute | solution.py:465
  12.0 1.3 %collective-permute-done.1 = s32[1,128]{1,0:T(1,128)S(1)} collective-permute-done((s32[1,128]{1,0:T(1,128)S(1)}, s32[1,128]{1,0:T(1,128)S(1)}, u32[]{:S(2)}, u32[]{:S(2)}) %collective-permute-start.1) | collective-permute-done | bytes 544 | tf_op jit(solution)/shard_map/ppermute | solution.py:465
  13.3 1.8 %collective-permute-start.2 = (s32[1,128]{1,0:T(1,128)S(1)}, s32[1,128]{1,0:T(1,128)S(1)}, u32[]{:S(2)}, u32[]{:S(2)}) collective-permute-start(s32[1,128]{1,0:T(1,128)S(1)} %add.31), channel_id=1, source_target_pairs={{0,5},{1,4},{2,7},{3,6},{4,1},{5,0},{6,3},{7,2},{8,13},{9,12},{10,... | collective-permute-start | bytes 1544 | tf_op jit(solution)/shard_map/ppermute | solution.py:465
  15.0 1.3 %collective-permute-done.2 = s32[1,128]{1,0:T(1,128)S(1)} collective-permute-done((s32[1,128]{1,0:T(1,128)S(1)}, s32[1,128]{1,0:T(1,128)S(1)}, u32[]{:S(2)}, u32[]{:S(2)}) %collective-permute-start.2) | collective-permute-done | bytes 544 | tf_op jit(solution)/shard_map/ppermute | solution.py:465
  16.3 2.7 %collective-permute-start.3 = (s32[1,128]{1,0:T(1,128)S(1)}, s32[1,128]{1,0:T(1,128)S(1)}, u32[]{:S(2)}, u32[]{:S(2)}) collective-permute-start(s32[1,128]{1,0:T(1,128)S(1)} %add.32), channel_id=1, source_target_pairs={{0,9},{1,8},{2,11},{3,10},{4,13},{5,12},{6,15},{7,14},{8,1},{9,0},... | collective-permute-start | bytes 1544 | tf_op jit(solution)/shard_map/ppermute | solution.py:465
  19.0 1.3 %collective-permute-done.3 = s32[1,128]{1,0:T(1,128)S(1)} collective-permute-done((s32[1,128]{1,0:T(1,128)S(1)}, s32[1,128]{1,0:T(1,128)S(1)}, u32[]{:S(2)}, u32[]{:S(2)}) %collective-permute-start.3) | collective-permute-done | bytes 544 | tf_op jit(solution)/shard_map/ppermute | solution.py:465
  20.3 0.0 collective-permute-done.4.other_ref
  20.3 0.0 copy-done
  20.3 0.3 slots.1
  20.6 2.6 %collective-permute-start.5 = (f32[2,56,128]{2,1,0:T(8,128)S(1)}, f32[2,56,128]{2,1,0:T(8,128)S(1)}, u32[]{:S(2)}, u32[]{:S(2)}) collective-permute-start(f32[2,56,128]{2,1,0:T(8,128)S(1)} %get-tuple-element.26), channel_id=1, source_target_pairs={{0,7},{1,6},{2,5},{3,4},{4,3},{5,2},{6,1},{7,0},{8,15},{9,14},{10,... | collective-permute-start | bytes 172040 | tf_op jit(solution)/shard_map/ppermute | solution.py:485
  23.2 0.2 collective-permute-start.6
  23.4 0.2 collective-permute-start.7
  23.6 1.9 %collective-permute-done.5 = f32[2,56,128]{2,1,0:T(8,128)S(1)} collective-permute-done((f32[2,56,128]{2,1,0:T(8,128)S(1)}, f32[2,56,128]{2,1,0:T(8,128)S(1)}, u32[]{:S(2)}, u32[]{:S(2)}) %collective-permute-start.5) | collective-permute-done | bytes 57376 | tf_op jit(solution)/shard_map/ppermute | solution.py:485
  25.5 1.6 %collective-permute-done.6 = f32[2,56,128]{2,1,0:T(8,128)S(1)} collective-permute-done((f32[2,56,128]{2,1,0:T(8,128)S(1)}, f32[2,56,128]{2,1,0:T(8,128)S(1)}, u32[]{:S(2)}, u32[]{:S(2)}) %collective-permute-start.6) | collective-permute-done | bytes 57376 | tf_op jit(solution)/shard_map/ppermute | solution.py:485
  27.1 0.1 collective-permute-done.7
  27.2 2.6 %collective-permute-start.8 = (f32[1,56,128]{2,1,0:T(8,128)S(1)}, f32[1,56,128]{2,1,0:T(8,128)S(1)}, u32[]{:S(2)}, u32[]{:S(2)}) collective-permute-start(f32[1,56,128]{2,1,0:T(8,128)S(1)} %get-tuple-element.29), channel_id=1, source_target_pairs={{0,9},{1,8},{2,11},{3,10},{4,13},{5,12},{6,15},{7,14},{8,1},{9,0},... | collective-permute-start | bytes 86024 | tf_op jit(solution)/shard_map/ppermute | solution.py:489
  29.8 1.7 %collective-permute-done.8.refs_0_ = f32[1,56,128]{2,1,0:T(8,128)S(1)} collective-permute-done((f32[1,56,128]{2,1,0:T(8,128)S(1)}, f32[1,56,128]{2,1,0:T(8,128)S(1)}, u32[]{:S(2)}, u32[]{:S(2)}) %collective-permute-start.8) | collective-permute-done | bytes 28704 | tf_op jit(solution)/shard_map/ppermute | solution.py:489
  31.4 0.0 copy-done.1
  31.4 0.0 copy-done.2
  31.4 0.9 %brick.1 = f32[1,4,2304]{2,1,0:T(4,128)} custom-call(f32[1,56,128]{2,1,0:T(8,128)S(1)} %get-tuple-element.30.mine_ref, f32[1,56,128]{2,1,0:T(8,128)S(1)} %collective-permute-done.8.refs_0_, f32[4,640]{1,0:T(4,128)S(1)} %copy-done.1, f32[4,640]{1,0:T(4,128)S(1)} %copy-done.2), custom_call_target="tpu_custom_call" | custom-call | tf_op jit(solution)/shard_map/brick/pallas_call | solution.py:420
  (6 shorter events, 0.0 us)
Async XLA Ops:
  5.4 14.9 %copy-start = (f32[16,56,128]{2,1,0:T(8,128)S(1)}, f32[16,56,128]{2,1,0:T(8,128)}, u32[]{:S(2)}) copy-start(f32[16,56,128]{2,1,0:T(8,128)} %constant.6.clone.window_ref) | copy-start | bytes 1376260
  6.9 24.6 %copy-start.1 = (f32[4,640]{1,0:T(4,128)S(1)}, f32[4,640]{1,0:T(4,128)}, u32[]{:S(2)}) copy-start(f32[4,640]{1,0:T(4,128)} %constant.7.clone.refs_1_) | copy-start | bytes 30724
  6.9 24.6 %copy-start.2 = (f32[4,640]{1,0:T(4,128)S(1)}, f32[4,640]{1,0:T(4,128)}, u32[]{:S(2)}) copy-start(f32[4,640]{1,0:T(4,128)} %constant.8.clone.refs_2_) | copy-start | bytes 30724
  6.9 13.4 %collective-permute-start.4 = (f32[16,56,128]{2,1,0:T(8,128)S(1)}, f32[16,56,128]{2,1,0:T(8,128)S(1)}, u32[]{:S(2)}, u32[]{:S(2)}) collective-permute-start(f32[16,56,128]{2,1,0:T(8,128)S(1)} %get-tuple-element.24.mine_ref), channel_id=1, source_target_pairs={{0,1},{1,0},{2,3},{3,2},{4,5},{5,4},{6,7},{7,6},{8,9},{9,8},{10,11... | collective-permute-start | bytes 1376264 | tf_op jit(solution)/shard_map/ppermute | solution.py:483
  8.1 1.2 %collective-permute-start = (s32[1,128]{1,0:T(1,128)S(1)}, s32[1,128]{1,0:T(1,128)S(1)}, u32[]{:S(2)}, u32[]{:S(2)}) collective-permute-start(s32[1,128]{1,0:T(1,128)S(1)} %seed.1), channel_id=1, source_target_pairs={{0,1},{1,0},{2,3},{3,2},{4,5},{5,4},{6,7},{7,6},{8,9},{9,8},{10,11... | collective-permute-start | bytes 1544 | tf_op jit(solution)/shard_map/ppermute | solution.py:465
  9.3 3.9 %collective-permute-start.1 = (s32[1,128]{1,0:T(1,128)S(1)}, s32[1,128]{1,0:T(1,128)S(1)}, u32[]{:S(2)}, u32[]{:S(2)}) collective-permute-start(s32[1,128]{1,0:T(1,128)S(1)} %add.30), channel_id=1, source_target_pairs={{0,3},{1,2},{2,1},{3,0},{4,7},{5,6},{6,5},{7,4},{8,11},{9,10},{10,... | collective-permute-start | bytes 1544 | tf_op jit(solution)/shard_map/ppermute | solution.py:465
  13.3 3.1 %collective-permute-start.2 = (s32[1,128]{1,0:T(1,128)S(1)}, s32[1,128]{1,0:T(1,128)S(1)}, u32[]{:S(2)}, u32[]{:S(2)}) collective-permute-start(s32[1,128]{1,0:T(1,128)S(1)} %add.31), channel_id=1, source_target_pairs={{0,5},{1,4},{2,7},{3,6},{4,1},{5,0},{6,3},{7,2},{8,13},{9,12},{10,... | collective-permute-start | bytes 1544 | tf_op jit(solution)/shard_map/ppermute | solution.py:465
  16.3 4.0 %collective-permute-start.3 = (s32[1,128]{1,0:T(1,128)S(1)}, s32[1,128]{1,0:T(1,128)S(1)}, u32[]{:S(2)}, u32[]{:S(2)}) collective-permute-start(s32[1,128]{1,0:T(1,128)S(1)} %add.32), channel_id=1, source_target_pairs={{0,9},{1,8},{2,11},{3,10},{4,13},{5,12},{6,15},{7,14},{8,1},{9,0},... | collective-permute-start | bytes 1544 | tf_op jit(solution)/shard_map/ppermute | solution.py:465
  20.6 4.9 %collective-permute-start.5 = (f32[2,56,128]{2,1,0:T(8,128)S(1)}, f32[2,56,128]{2,1,0:T(8,128)S(1)}, u32[]{:S(2)}, u32[]{:S(2)}) collective-permute-start(f32[2,56,128]{2,1,0:T(8,128)S(1)} %get-tuple-element.26), channel_id=1, source_target_pairs={{0,7},{1,6},{2,5},{3,4},{4,3},{5,2},{6,1},{7,0},{8,15},{9,14},{10,... | collective-permute-start | bytes 172040 | tf_op jit(solution)/shard_map/ppermute | solution.py:485
  23.2 3.9 %collective-permute-start.6 = (f32[2,56,128]{2,1,0:T(8,128)S(1)}, f32[2,56,128]{2,1,0:T(8,128)S(1)}, u32[]{:S(2)}, u32[]{:S(2)}) collective-permute-start(f32[2,56,128]{2,1,0:T(8,128)S(1)} %get-tuple-element.27), channel_id=1, source_target_pairs={{0,5},{1,4},{2,7},{3,6},{4,1},{5,0},{6,3},{7,2},{8,13},{9,12},{10,... | collective-permute-start | bytes 172040 | tf_op jit(solution)/shard_map/ppermute | solution.py:485
  23.4 3.7 %collective-permute-start.7 = (f32[2,56,128]{2,1,0:T(8,128)S(1)}, f32[2,56,128]{2,1,0:T(8,128)S(1)}, u32[]{:S(2)}, u32[]{:S(2)}) collective-permute-start(f32[2,56,128]{2,1,0:T(8,128)S(1)} %get-tuple-element.28), channel_id=1, source_target_pairs={{0,3},{1,2},{2,1},{3,0},{4,7},{5,6},{6,5},{7,4},{8,11},{9,10},{10,... | collective-permute-start | bytes 172040 | tf_op jit(solution)/shard_map/ppermute | solution.py:485
  27.2 4.3 %collective-permute-start.8 = (f32[1,56,128]{2,1,0:T(8,128)S(1)}, f32[1,56,128]{2,1,0:T(8,128)S(1)}, u32[]{:S(2)}, u32[]{:S(2)}) collective-permute-start(f32[1,56,128]{2,1,0:T(8,128)S(1)} %get-tuple-element.29), channel_id=1, source_target_pairs={{0,9},{1,8},{2,11},{3,10},{4,13},{5,12},{6,15},{7,14},{8,1},{9,0},... | collective-permute-start | bytes 86024 | tf_op jit(solution)/shard_map/ppermute | solution.py:489

commit v3 on v2

--- a/solution.py
+++ b/solution.py
@@ -17,7 +17,7 @@
 PAD = 32
 LANES = 128
 CHUNKS = 2
-FAR_FIRST = (3, 2, 1)
+START_ORDER = (1, 3, 2)
 DIRECT = 2
 LEAD = 1
 SPARE = 96
@@ -160,8 +160,7 @@
 
 def patch_kernel(half, tiles, brick_rows, keep_from, last, aug_ref, xs_ref, plane_ref, depth_ref, head_ref, *refs):
     if last:
-        carry_in, _, anchor_ref, out_ref, anchor_out, a_ref = refs
-        anchor_out[...] = jnp.full(anchor_out.shape, anchor_ref[0], I32)
+        carry_in, _, out_ref, a_ref = refs
     else:
         out_ref, carry_out, a_ref = refs
     rows, _ = xs_ref.shape
@@ -285,13 +284,12 @@
     kept = head.shape[0]
     carried = extra[0].shape[0] if last else 0
     bricks = jax.ShapeDtypeStruct((16, kept + 8, LANES), F32)
-    beside = jax.ShapeDtypeStruct((1, LANES), I32) if last else jax.ShapeDtypeStruct((2 * len(tiles) - keep_from, kept, LANES), F32)
-    spaces = [vmem(), vmem(), smem()] if last else []
+    beside = jax.ShapeDtypeStruct((2 * len(tiles) - keep_from, kept, LANES), F32)
     return pl.pallas_call(
         functools.partial(patch_kernel, half, tiles, brick_rows, keep_from, last),
-        out_shape=[bricks, beside],
-        in_specs=[smem()] + [vmem()] * 4 + spaces,
-        out_specs=[vmem()] * 2,
+        out_shape=[bricks] if last else [bricks, beside],
+        in_specs=[smem()] + [vmem()] * (4 + len(extra)),
+        out_specs=[vmem()] * (1 if last else 2),
         scratch_shapes=[pltpu.VMEM((2 * len(tiles) + carried, kept, LANES), F32)],
         input_output_aliases={6: 0} if last else {},
         compiler_params=params(),
@@ -324,7 +322,7 @@
     me = lax.axis_index("patch")
     brick_rows = devices // 4
     brick = iota(table_ref.shape, 1)
-    row = lax.rem(brick // 4 - anchor_ref[:, :1] + brick_rows, jnp.full_like(brick, brick_rows))
+    row = lax.rem(brick // 4 - anchor_ref[0] + brick_rows, jnp.full_like(brick, brick_rows))
     place = row * 4 + brick % 4
     owner = jnp.where(brick < devices, table_ref[...], -1)
     _, rows, lanes = mine_ref.shape
@@ -347,7 +345,7 @@
     return pl.pallas_call(
         functools.partial(slots_kernel, devices, masks),
         out_shape=[shape] * pieces,
-        in_specs=[vmem()] * 5,
+        in_specs=[vmem(), smem()] + [vmem()] * 3,
         out_specs=[vmem()] * pieces,
         compiler_params=params(),
         name="slots",
@@ -461,13 +459,13 @@
         masks = masks + [bit ^ mask for mask in masks]
     masks = [first ^ mask for first in direct for mask in masks]
 
-    def table_round(k, table):
-        return table + lax.ppermute(table, "patch", partner(devices, rounds[k]))
-
-    rounds = paired
     table = seed_table(brick_owner, devices)
-    for k in range(len(rounds)):
-        table = table_round(k, table)
+    near = []
+    for mask in (1, 3, 2):
+        near.append(lax.ppermute(table, "patch", partner(devices, mask)))
+    table = functools.reduce(lambda a, b: a + b, near, table)
+    for bit in paired[2:]:
+        table = table + lax.ppermute(table, "patch", partner(devices, bit))
     plane, depth_w, head, shifted = front(aug_code, w_in, w_plane, w_depth, w_head, features[0])
     half = math.isqrt(cells)
     steps = cells // (2 * LANES)
@@ -477,12 +475,12 @@
     early = [i for i in range(4) if starts[i] + span < 2 * ready]
     late = [i for i in range(4) if i not in early]
     bricks, carry = patch_half(half, range(ready), early, starts[late[0]], False, aug_code, shifted, plane, depth_w, head)
-    bricks, anchor = patch_half(
-        half, range(ready, steps), late, 0, True, aug_code, shifted, plane, depth_w, head, (carry, bricks, patch_anchor)
+    (bricks,) = patch_half(
+        half, range(ready, steps), late, 0, True, aug_code, shifted, plane, depth_w, head, (carry, bricks)
     )
     other = lax.ppermute(bricks, "patch", partner(devices, 1))
-    parts = fill_slots(devices, masks, len(direct), table, anchor, bricks, other, wire_window(side, maps, depth))
-    sums = [parts[0]] + [lax.ppermute(parts[q], "patch", partner(devices, direct[q])) for q in FAR_FIRST]
+    parts = fill_slots(devices, masks, len(direct), table, patch_anchor, bricks, other, wire_window(side, maps, depth))
+    sums = [parts[0]] + [lax.ppermute(parts[q], "patch", partner(devices, direct[q])) for q in START_ORDER]
     for bit in halved:
         size = sums[0].shape[0] // 2
         keep, send = (functools.reduce(lambda a, b: a + b, [one[k : k + size] for one in sums]) for k in (0, size))

time: 32.5 us -> 33.4 us (1.028)
  waiting for transfers between devices: 10.2 us -> 13.5 us
  starting transfers between devices: 13.4 us -> 11 us
    ppermute x4 -> x5, waiting for transfers between devices: 5.03 us -> 6.87 us  [the longest x2 3.63 us: on_device(): table = table + lax.ppermute(table, 'patch', partner(devices, bit))]
    ppermute x4 -> x5, starting transfers between devices: 7.17 us -> 5.69 us  [the longest x3 3.08 us: on_device(): near.append(lax.ppermute(table, 'patch', partner(devices, mask)))]
    ppermute x1, waiting for transfers between devices: 1.65 us -> 2.77 us  [on_device(): sums = [keep, lax.ppermute(send, 'patch', partner(devices, bit))]]
    ppermute x1, starting transfers between devices: 2.61 us -> 1.82 us  [on_device(): sums = [keep, lax.ppermute(send, 'patch', partner(devices, bit))]]
    ppermute x3, waiting for transfers between devices: 3.5 us -> 3.87 us  [on_device(): lax.ppermute(parts[q], 'patch', partner(devices, direct[q]))]
  transfers between devices with their start and end apart: 9 -> 10, of which waited for: 8 -> 8; matrix products, arithmetic and copies ran while one was open for 0% -> 0% of each run, Pallas kernels for 0% -> 0%
where the time goes in v3:
time: 33.4 us; the launch traced here: 33.2 us
  waiting for transfers between devices  13.5 us (40%)
  starting transfers between devices  11 us (33%)
  Pallas kernels  6.63 us (20%)
  between operations  2.03 us (6%)
    ppermute x3, waiting for transfers between devices, on_device(): lax.ppermute(parts[q], 'patch', partner(devices, direct[q]))  3.87 us
    pallas_call x2, Pallas kernels, patch_half(): pl.pallas_call(functools.partial(patch_kernel, half, tiles, brick_rows, k...  3.66 us
    ppermute x2, waiting for transfers between devices, on_device(): table = table + lax.ppermute(table, 'patch', partner(devices, bit))  3.63 us
    ppermute x3, waiting for transfers between devices, on_device(): near.append(lax.ppermute(table, 'patch', partner(devices, mask)))  3.25 us
    ppermute x3, starting transfers between devices, on_device(): near.append(lax.ppermute(table, 'patch', partner(devices, mask)))  3.08 us
    ppermute x3, starting transfers between devices, on_device(): lax.ppermute(parts[q], 'patch', partner(devices, direct[q]))  2.93 us
    ppermute x1, waiting for transfers between devices, on_device(): sums = [keep, lax.ppermute(send, 'patch', partner(devices, bit))]  2.77 us
    ppermute x2, starting transfers between devices, on_device(): table = table + lax.ppermute(table, 'patch', partner(devices, bit))  2.61 us
  transfers between devices with their start and end apart: 10, of which 8 were waited for; matrix products, arithmetic and copies ran while one was open for 0% of the time, Pallas kernels for 0%

profile of v3, /device:TPU:0, one launch (start us, length us, event | category | flops | bytes accessed | tf_op | source)
XLA Modules:
  0.0 33.2 jit_solution(9464118633844713554)
XLA Ops:
  0.7 1.9 %front.1 = (bf16[2,128,192]{2,1,0:T(8,128)(2,1)S(1)}, bf16[128,128]{1,0:T(8,128)(2,1)S(1)}, bf16[48,512]{1,0:T(8,128)(2,1)S(1)}, bf16[128,2560]{1,0:T(8,128)(2,1)S(1)}) custom-call(s32[1]{0:T(128)S(6)} %copy.16.aug_ref, bf16[28,64]{1,0:T(8,128)(2,1)} %w_in_hbm.1, bf16[9,28,28]{2,1,0:T(8,128)(2,1)} %w_plane_hbm.1, bf16[3,28,28]{2,1,0:T(8,128)(2,1)} %w_depth_hbm.1, ...), custom_call_target="tpu_custom_call" | custom-call | flops 100000000 | bytes 1048576 | tf_op jit(solution)/shard_map/front/pallas_call | solution.py:139
  2.5 2.2 %shard_map.109 = (f32[16,56,128]{2,1,0:T(8,128)S(1)}, f32[3,48,128]{2,1,0:T(8,128)S(1)}) custom-call(s32[1]{0:T(128)S(6)} %copy.16.aug_ref, bf16[128,2560]{1,0:T(8,128)(2,1)S(1)} %get-tuple-element.15.xs_ref, bf16[2,128,192]{2,1,0:T(8,128)(2,1)S(1)} %get-tuple-element.16.plane_ref, bf16[128,128]{1,0:T(8,128)(2,1)S(1)} %get-tuple-element.17.depth_ref, ...), custom_call_target="tpu_custom_call" | custom-call | flops 1000000000 | bytes 1048576 | tf_op jit(solution)/shard_map/pallas_call | solution.py:288
  4.8 0.0 copy-start
  4.8 1.4 %shard_map.110.mine_ref = f32[16,56,128]{2,1,0:T(8,128)S(1)} custom-call(s32[1]{0:T(128)S(6)} %copy.16.aug_ref, bf16[128,2560]{1,0:T(8,128)(2,1)S(1)} %get-tuple-element.15.xs_ref, bf16[2,128,192]{2,1,0:T(8,128)(2,1)S(1)} %get-tuple-element.16.plane_ref, bf16[128,128]{1,0:T(8,128)(2,1)S(1)} %get-tuple-element.17.depth_ref, ...), custom_call_target="tpu_custom_call", output_to_operand_aliasing={{}: (6, {})} | custom-call | flops 1000000000 | bytes 1048576 | tf_op jit(solution)/shard_map/pallas_call | solution.py:288
  6.2 0.0 copy-start.1
  6.2 0.0 copy-start.2
  6.2 0.6 %collective-permute-start.5 = (f32[16,56,128]{2,1,0:T(8,128)S(1)}, f32[16,56,128]{2,1,0:T(8,128)S(1)}, u32[]{:S(2)}, u32[]{:S(2)}) collective-permute-start(f32[16,56,128]{2,1,0:T(8,128)S(1)} %shard_map.110.mine_ref), channel_id=1, source_target_pairs={{0,1},{1,0},{2,3},{3,2},{4,5},{5,4},{6,7},{7,6},{8,9},{9,8},{10,11... | collective-permute-start | bytes 1376264 | tf_op jit(solution)/shard_map/ppermute | solution.py:481
  7.5 0.1 collective-permute-start
  7.6 2.7 %collective-permute-start.1 = (s32[1,128]{1,0:T(1,128)S(1)}, s32[1,128]{1,0:T(1,128)S(1)}, u32[]{:S(2)}, u32[]{:S(2)}) collective-permute-start(s32[1,128]{1,0:T(1,128)S(1)} %seed.1), channel_id=1, source_target_pairs={{0,3},{1,2},{2,1},{3,0},{4,7},{5,6},{6,5},{7,4},{8,11},{9,10},{10,... | collective-permute-start | bytes 1544 | tf_op jit(solution)/shard_map/ppermute | solution.py:465
  10.2 0.3 collective-permute-start.2
  10.6 0.0 collective-permute-done
  10.6 1.0 %collective-permute-done.1 = s32[1,128]{1,0:T(1,128)S(1)} collective-permute-done((s32[1,128]{1,0:T(1,128)S(1)}, s32[1,128]{1,0:T(1,128)S(1)}, u32[]{:S(2)}, u32[]{:S(2)}) %collective-permute-start.1) | collective-permute-done | bytes 544 | tf_op jit(solution)/shard_map/ppermute | solution.py:465
  11.5 2.3 %collective-permute-done.2 = s32[1,128]{1,0:T(1,128)S(1)} collective-permute-done((s32[1,128]{1,0:T(1,128)S(1)}, s32[1,128]{1,0:T(1,128)S(1)}, u32[]{:S(2)}, u32[]{:S(2)}) %collective-permute-start.2) | collective-permute-done | bytes 544 | tf_op jit(solution)/shard_map/ppermute | solution.py:465
  13.8 0.5 %collective-permute-start.3 = (s32[1,128]{1,0:T(1,128)S(1)}, s32[1,128]{1,0:T(1,128)S(1)}, u32[]{:S(2)}, u32[]{:S(2)}) collective-permute-start(s32[1,128]{1,0:T(1,128)S(1)} %add_add_fusion), channel_id=1, source_target_pairs={{0,5},{1,4},{2,7},{3,6},{4,1},{5,0},{6,3},{7,2},{8,13},{9,12},{10,... | collective-permute-start | bytes 1544 | tf_op jit(solution)/shard_map/ppermute | solution.py:468
  14.3 2.5 %collective-permute-done.3 = s32[1,128]{1,0:T(1,128)S(1)} collective-permute-done((s32[1,128]{1,0:T(1,128)S(1)}, s32[1,128]{1,0:T(1,128)S(1)}, u32[]{:S(2)}, u32[]{:S(2)}) %collective-permute-start.3) | collective-permute-done | bytes 544 | tf_op jit(solution)/shard_map/ppermute | solution.py:468
  16.8 2.1 %collective-permute-start.4 = (s32[1,128]{1,0:T(1,128)S(1)}, s32[1,128]{1,0:T(1,128)S(1)}, u32[]{:S(2)}, u32[]{:S(2)}) collective-permute-start(s32[1,128]{1,0:T(1,128)S(1)} %add.36), channel_id=1, source_target_pairs={{0,9},{1,8},{2,11},{3,10},{4,13},{5,12},{6,15},{7,14},{8,1},{9,0},... | collective-permute-start | bytes 1544 | tf_op jit(solution)/shard_map/ppermute | solution.py:468
  19.6 1.1 %collective-permute-done.4 = s32[1,128]{1,0:T(1,128)S(1)} collective-permute-done((s32[1,128]{1,0:T(1,128)S(1)}, s32[1,128]{1,0:T(1,128)S(1)}, u32[]{:S(2)}, u32[]{:S(2)}) %collective-permute-start.4) | collective-permute-done | bytes 544 | tf_op jit(solution)/shard_map/ppermute | solution.py:468
  20.7 0.0 collective-permute-done.5.other_ref
  20.7 0.0 copy-done
  20.7 0.2 slots.1
  20.9 0.2 collective-permute-start.6
  21.2 2.6 %collective-permute-start.7 = (f32[2,56,128]{2,1,0:T(8,128)S(1)}, f32[2,56,128]{2,1,0:T(8,128)S(1)}, u32[]{:S(2)}, u32[]{:S(2)}) collective-permute-start(f32[2,56,128]{2,1,0:T(8,128)S(1)} %get-tuple-element.23), channel_id=1, source_target_pairs={{0,7},{1,6},{2,5},{3,4},{4,3},{5,2},{6,1},{7,0},{8,15},{9,14},{10,... | collective-permute-start | bytes 172040 | tf_op jit(solution)/shard_map/ppermute | solution.py:483
  23.8 0.1 collective-permute-start.8
  23.9 1.1 %collective-permute-done.6 = f32[2,56,128]{2,1,0:T(8,128)S(1)} collective-permute-done((f32[2,56,128]{2,1,0:T(8,128)S(1)}, f32[2,56,128]{2,1,0:T(8,128)S(1)}, u32[]{:S(2)}, u32[]{:S(2)}) %collective-permute-start.6) | collective-permute-done | bytes 57376 | tf_op jit(solution)/shard_map/ppermute | solution.py:483
  25.0 1.1 %collective-permute-done.7 = f32[2,56,128]{2,1,0:T(8,128)S(1)} collective-permute-done((f32[2,56,128]{2,1,0:T(8,128)S(1)}, f32[2,56,128]{2,1,0:T(8,128)S(1)}, u32[]{:S(2)}, u32[]{:S(2)}) %collective-permute-start.7) | collective-permute-done | bytes 57376 | tf_op jit(solution)/shard_map/ppermute | solution.py:483
  26.1 1.7 %collective-permute-done.8 = f32[2,56,128]{2,1,0:T(8,128)S(1)} collective-permute-done((f32[2,56,128]{2,1,0:T(8,128)S(1)}, f32[2,56,128]{2,1,0:T(8,128)S(1)}, u32[]{:S(2)}, u32[]{:S(2)}) %collective-permute-start.8) | collective-permute-done | bytes 57376 | tf_op jit(solution)/shard_map/ppermute | solution.py:483
  27.8 1.8 %collective-permute-start.9 = (f32[1,56,128]{2,1,0:T(8,128)S(1)}, f32[1,56,128]{2,1,0:T(8,128)S(1)}, u32[]{:S(2)}, u32[]{:S(2)}) collective-permute-start(f32[1,56,128]{2,1,0:T(8,128)S(1)} %get-tuple-element.25), channel_id=1, source_target_pairs={{0,9},{1,8},{2,11},{3,10},{4,13},{5,12},{6,15},{7,14},{8,1},{9,0},... | collective-permute-start | bytes 86024 | tf_op jit(solution)/shard_map/ppermute | solution.py:487
  29.6 2.8 %collective-permute-done.9.refs_0_ = f32[1,56,128]{2,1,0:T(8,128)S(1)} collective-permute-done((f32[1,56,128]{2,1,0:T(8,128)S(1)}, f32[1,56,128]{2,1,0:T(8,128)S(1)}, u32[]{:S(2)}, u32[]{:S(2)}) %collective-permute-start.9) | collective-permute-done | bytes 28704 | tf_op jit(solution)/shard_map/ppermute | solution.py:487
  32.3 0.0 copy-done.1
  32.4 0.0 copy-done.2
  32.4 0.9 %brick.1 = f32[1,4,2304]{2,1,0:T(4,128)} custom-call(f32[1,56,128]{2,1,0:T(8,128)S(1)} %get-tuple-element.26.mine_ref, f32[1,56,128]{2,1,0:T(8,128)S(1)} %collective-permute-done.9.refs_0_, f32[4,640]{1,0:T(4,128)S(1)} %copy-done.1, f32[4,640]{1,0:T(4,128)S(1)} %copy-done.2), custom_call_target="tpu_custom_call" | custom-call | tf_op jit(solution)/shard_map/brick/pallas_call | solution.py:418
  (5 shorter events, 0.0 us)
Async XLA Ops:
  4.8 15.9 %copy-start = (f32[16,56,128]{2,1,0:T(8,128)S(1)}, f32[16,56,128]{2,1,0:T(8,128)}, u32[]{:S(2)}) copy-start(f32[16,56,128]{2,1,0:T(8,128)} %constant.6.clone.window_ref) | copy-start | bytes 1376260
  6.2 26.1 %copy-start.1 = (f32[4,640]{1,0:T(4,128)S(1)}, f32[4,640]{1,0:T(4,128)}, u32[]{:S(2)}) copy-start(f32[4,640]{1,0:T(4,128)} %constant.7.clone.refs_1_) | copy-start | bytes 30724
  6.2 26.1 %copy-start.2 = (f32[4,640]{1,0:T(4,128)S(1)}, f32[4,640]{1,0:T(4,128)}, u32[]{:S(2)}) copy-start(f32[4,640]{1,0:T(4,128)} %constant.8.clone.refs_2_) | copy-start | bytes 30724
  6.2 14.5 %collective-permute-start.5 = (f32[16,56,128]{2,1,0:T(8,128)S(1)}, f32[16,56,128]{2,1,0:T(8,128)S(1)}, u32[]{:S(2)}, u32[]{:S(2)}) collective-permute-start(f32[16,56,128]{2,1,0:T(8,128)S(1)} %shard_map.110.mine_ref), channel_id=1, source_target_pairs={{0,1},{1,0},{2,3},{3,2},{4,5},{5,4},{6,7},{7,6},{8,9},{9,8},{10,11... | collective-permute-start | bytes 1376264 | tf_op jit(solution)/shard_map/ppermute | solution.py:481
  7.5 3.1 %collective-permute-start = (s32[1,128]{1,0:T(1,128)S(1)}, s32[1,128]{1,0:T(1,128)S(1)}, u32[]{:S(2)}, u32[]{:S(2)}) collective-permute-start(s32[1,128]{1,0:T(1,128)S(1)} %seed.1), channel_id=1, source_target_pairs={{0,1},{1,0},{2,3},{3,2},{4,5},{5,4},{6,7},{7,6},{8,9},{9,8},{10,11... | collective-permute-start | bytes 1544 | tf_op jit(solution)/shard_map/ppermute | solution.py:465
  7.6 4.0 %collective-permute-start.1 = (s32[1,128]{1,0:T(1,128)S(1)}, s32[1,128]{1,0:T(1,128)S(1)}, u32[]{:S(2)}, u32[]{:S(2)}) collective-permute-start(s32[1,128]{1,0:T(1,128)S(1)} %seed.1), channel_id=1, source_target_pairs={{0,3},{1,2},{2,1},{3,0},{4,7},{5,6},{6,5},{7,4},{8,11},{9,10},{10,... | collective-permute-start | bytes 1544 | tf_op jit(solution)/shard_map/ppermute | solution.py:465
  10.2 3.6 %collective-permute-start.2 = (s32[1,128]{1,0:T(1,128)S(1)}, s32[1,128]{1,0:T(1,128)S(1)}, u32[]{:S(2)}, u32[]{:S(2)}) collective-permute-start(s32[1,128]{1,0:T(1,128)S(1)} %seed.1), channel_id=1, source_target_pairs={{0,2},{1,3},{2,0},{3,1},{4,6},{5,7},{6,4},{7,5},{8,10},{9,11},{10,... | collective-permute-start | bytes 1544 | tf_op jit(solution)/shard_map/ppermute | solution.py:465
  13.8 3.0 %collective-permute-start.3 = (s32[1,128]{1,0:T(1,128)S(1)}, s32[1,128]{1,0:T(1,128)S(1)}, u32[]{:S(2)}, u32[]{:S(2)}) collective-permute-start(s32[1,128]{1,0:T(1,128)S(1)} %add_add_fusion), channel_id=1, source_target_pairs={{0,5},{1,4},{2,7},{3,6},{4,1},{5,0},{6,3},{7,2},{8,13},{9,12},{10,... | collective-permute-start | bytes 1544 | tf_op jit(solution)/shard_map/ppermute | solution.py:468
  16.8 3.9 %collective-permute-start.4 = (s32[1,128]{1,0:T(1,128)S(1)}, s32[1,128]{1,0:T(1,128)S(1)}, u32[]{:S(2)}, u32[]{:S(2)}) collective-permute-start(s32[1,128]{1,0:T(1,128)S(1)} %add.36), channel_id=1, source_target_pairs={{0,9},{1,8},{2,11},{3,10},{4,13},{5,12},{6,15},{7,14},{8,1},{9,0},... | collective-permute-start | bytes 1544 | tf_op jit(solution)/shard_map/ppermute | solution.py:468
  20.9 4.0 %collective-permute-start.6 = (f32[2,56,128]{2,1,0:T(8,128)S(1)}, f32[2,56,128]{2,1,0:T(8,128)S(1)}, u32[]{:S(2)}, u32[]{:S(2)}) collective-permute-start(f32[2,56,128]{2,1,0:T(8,128)S(1)} %get-tuple-element.22), channel_id=1, source_target_pairs={{0,3},{1,2},{2,1},{3,0},{4,7},{5,6},{6,5},{7,4},{8,11},{9,10},{10,... | collective-permute-start | bytes 172040 | tf_op jit(solution)/shard_map/ppermute | solution.py:483
  21.2 4.9 %collective-permute-start.7 = (f32[2,56,128]{2,1,0:T(8,128)S(1)}, f32[2,56,128]{2,1,0:T(8,128)S(1)}, u32[]{:S(2)}, u32[]{:S(2)}) collective-permute-start(f32[2,56,128]{2,1,0:T(8,128)S(1)} %get-tuple-element.23), channel_id=1, source_target_pairs={{0,7},{1,6},{2,5},{3,4},{4,3},{5,2},{6,1},{7,0},{8,15},{9,14},{10,... | collective-permute-start | bytes 172040 | tf_op jit(solution)/shard_map/ppermute | solution.py:483
  23.8 4.0 %collective-permute-start.8 = (f32[2,56,128]{2,1,0:T(8,128)S(1)}, f32[2,56,128]{2,1,0:T(8,128)S(1)}, u32[]{:S(2)}, u32[]{:S(2)}) collective-permute-start(f32[2,56,128]{2,1,0:T(8,128)S(1)} %get-tuple-element.24), channel_id=1, source_target_pairs={{0,5},{1,4},{2,7},{3,6},{4,1},{5,0},{6,3},{7,2},{8,13},{9,12},{10,... | collective-permute-start | bytes 172040 | tf_op jit(solution)/shard_map/ppermute | solution.py:483
  27.8 4.6 %collective-permute-start.9 = (f32[1,56,128]{2,1,0:T(8,128)S(1)}, f32[1,56,128]{2,1,0:T(8,128)S(1)}, u32[]{:S(2)}, u32[]{:S(2)}) collective-permute-start(f32[1,56,128]{2,1,0:T(8,128)S(1)} %get-tuple-element.25), channel_id=1, source_target_pairs={{0,9},{1,8},{2,11},{3,10},{4,13},{5,12},{6,15},{7,14},{8,1},{9,0},... | collective-permute-start | bytes 86024 | tf_op jit(solution)/shard_map/ppermute | solution.py:487

commit v4 on v3

--- a/solution.py
+++ b/solution.py
@@ -19,7 +19,7 @@
 CHUNKS = 2
 START_ORDER = (1, 3, 2)
 DIRECT = 2
-LEAD = 1
+LEAD = 2
 SPARE = 96
 
 
@@ -459,13 +459,13 @@
         masks = masks + [bit ^ mask for mask in masks]
     masks = [first ^ mask for first in direct for mask in masks]
 
+    def table_round(k, table):
+        return table + lax.ppermute(table, "patch", partner(devices, rounds[k]))
+
+    rounds = paired
     table = seed_table(brick_owner, devices)
-    near = []
-    for mask in (1, 3, 2):
-        near.append(lax.ppermute(table, "patch", partner(devices, mask)))
-    table = functools.reduce(lambda a, b: a + b, near, table)
-    for bit in paired[2:]:
-        table = table + lax.ppermute(table, "patch", partner(devices, bit))
+    for k in range(len(rounds)):
+        table = table_round(k, table)
     plane, depth_w, head, shifted = front(aug_code, w_in, w_plane, w_depth, w_head, features[0])
     half = math.isqrt(cells)
     steps = cells // (2 * LANES)

time: 33.4 us -> 31.8 us (0.952)
  waiting for transfers between devices: 13.5 us -> 9.61 us
  starting transfers between devices: 11 us -> 13.3 us
    ppermute x5 -> x4, waiting for transfers between devices: 6.87 us -> 4.38 us  [table_round(): return table + lax.ppermute(table, 'patch', partner(devices, rounds[k]))]
    ppermute x5 -> x4, starting transfers between devices: 5.69 us -> 7.17 us  [table_round(): return table + lax.ppermute(table, 'patch', partner(devices, rounds[k]))]
    ppermute x1, waiting for transfers between devices: 2.77 us -> 1.65 us  [on_device(): sums = [keep, lax.ppermute(send, 'patch', partner(devices, bit))]]
    ppermute x1, starting transfers between devices: 1.82 us -> 2.61 us  [on_device(): sums = [keep, lax.ppermute(send, 'patch', partner(devices, bit))]]
  transfers between devices with their start and end apart: 10 -> 9, of which waited for: 8 -> 8; matrix products, arithmetic and copies ran while one was open for 0% -> 0% of each run, Pallas kernels for 0% -> 0%
where the time goes in v4:
time: 31.8 us; the launch traced here: 31.6 us
  starting transfers between devices  13.3 us (42%)
  waiting for transfers between devices  9.61 us (30%)
  Pallas kernels  6.62 us (21%)
  between operations  2.04 us (6%)
    ppermute x4, starting transfers between devices, table_round(): return table + lax.ppermute(table, 'patch', partner(devices, rounds[k]))  7.17 us
    ppermute x4, waiting for transfers between devices, table_round(): return table + lax.ppermute(table, 'patch', partner(devices, rounds[k]))  4.38 us
    pallas_call x2, Pallas kernels, patch_half(): pl.pallas_call(functools.partial(patch_kernel, half, tiles, brick_rows, k...  3.65 us
    ppermute x3, waiting for transfers between devices, on_device(): lax.ppermute(parts[q], 'patch', partner(devices, direct[q]))  3.57 us
    ppermute x3, starting transfers between devices, on_device(): lax.ppermute(parts[q], 'patch', partner(devices, direct[q]))  3 us
    ppermute x1, starting transfers between devices, on_device(): sums = [keep, lax.ppermute(send, 'patch', partner(devices, bit))]  2.61 us
    pallas_call x1, Pallas kernels, front(): pl.pallas_call(front_kernel, out_shape=[jax.ShapeDtypeStruct(s, BF16) for...  1.87 us
    ppermute x1, waiting for transfers between devices, on_device(): sums = [keep, lax.ppermute(send, 'patch', partner(devices, bit))]  1.65 us
  transfers between devices with their start and end apart: 9, of which 8 were waited for; matrix products, arithmetic and copies ran while one was open for 0% of the time, Pallas kernels for 0%

profile of v4, /device:TPU:0, one launch (start us, length us, event | category | flops | bytes accessed | tf_op | source)
XLA Modules:
  0.0 31.6 jit_solution(7644710838226221803)
XLA Ops:
  0.7 1.9 %front.1 = (bf16[2,128,192]{2,1,0:T(8,128)(2,1)S(1)}, bf16[128,128]{1,0:T(8,128)(2,1)S(1)}, bf16[48,512]{1,0:T(8,128)(2,1)S(1)}, bf16[128,2560]{1,0:T(8,128)(2,1)S(1)}) custom-call(s32[1]{0:T(128)S(6)} %copy.16.aug_ref, bf16[28,64]{1,0:T(8,128)(2,1)} %w_in_hbm.1, bf16[9,28,28]{2,1,0:T(8,128)(2,1)} %w_plane_hbm.1, bf16[3,28,28]{2,1,0:T(8,128)(2,1)} %w_depth_hbm.1, ...), custom_call_target="tpu_custom_call" | custom-call | flops 100000000 | bytes 1048576 | tf_op jit(solution)/shard_map/front/pallas_call | solution.py:139
  2.5 2.5 %shard_map.109 = (f32[16,56,128]{2,1,0:T(8,128)S(1)}, f32[5,48,128]{2,1,0:T(8,128)S(1)}) custom-call(s32[1]{0:T(128)S(6)} %copy.16.aug_ref, bf16[128,2560]{1,0:T(8,128)(2,1)S(1)} %get-tuple-element.15.xs_ref, bf16[2,128,192]{2,1,0:T(8,128)(2,1)S(1)} %get-tuple-element.16.plane_ref, bf16[128,128]{1,0:T(8,128)(2,1)S(1)} %get-tuple-element.17.depth_ref, ...), custom_call_target="tpu_custom_call" | custom-call | flops 1000000000 | bytes 1048576 | tf_op jit(solution)/shard_map/pallas_call | solution.py:288
  5.0 0.0 copy-start
  5.0 1.2 %shard_map.110.mine_ref = f32[16,56,128]{2,1,0:T(8,128)S(1)} custom-call(s32[1]{0:T(128)S(6)} %copy.16.aug_ref, bf16[128,2560]{1,0:T(8,128)(2,1)S(1)} %get-tuple-element.15.xs_ref, bf16[2,128,192]{2,1,0:T(8,128)(2,1)S(1)} %get-tuple-element.16.plane_ref, bf16[128,128]{1,0:T(8,128)(2,1)S(1)} %get-tuple-element.17.depth_ref, ...), custom_call_target="tpu_custom_call", output_to_operand_aliasing={{}: (6, {})} | custom-call | flops 1000000000 | bytes 1048576 | tf_op jit(solution)/shard_map/pallas_call | solution.py:288
  6.2 0.0 copy-start.1
  6.2 0.0 copy-start.2
  6.2 0.6 %collective-permute-start.4 = (f32[16,56,128]{2,1,0:T(8,128)S(1)}, f32[16,56,128]{2,1,0:T(8,128)S(1)}, u32[]{:S(2)}, u32[]{:S(2)}) collective-permute-start(f32[16,56,128]{2,1,0:T(8,128)S(1)} %shard_map.110.mine_ref), channel_id=1, source_target_pairs={{0,1},{1,0},{2,3},{3,2},{4,5},{5,4},{6,7},{7,6},{8,9},{9,8},{10,11... | collective-permute-start | bytes 1376264 | tf_op jit(solution)/shard_map/ppermute | solution.py:481
  7.5 0.1 collective-permute-start
  7.5 1.1 %collective-permute-done = s32[1,128]{1,0:T(1,128)S(1)} collective-permute-done((s32[1,128]{1,0:T(1,128)S(1)}, s32[1,128]{1,0:T(1,128)S(1)}, u32[]{:S(2)}, u32[]{:S(2)}) %collective-permute-start) | collective-permute-done | bytes 544 | tf_op jit(solution)/shard_map/ppermute | solution.py:463
  8.7 2.6 %collective-permute-start.1 = (s32[1,128]{1,0:T(1,128)S(1)}, s32[1,128]{1,0:T(1,128)S(1)}, u32[]{:S(2)}, u32[]{:S(2)}) collective-permute-start(s32[1,128]{1,0:T(1,128)S(1)} %add.30), channel_id=1, source_target_pairs={{0,3},{1,2},{2,1},{3,0},{4,7},{5,6},{6,5},{7,4},{8,11},{9,10},{10,... | collective-permute-start | bytes 1544 | tf_op jit(solution)/shard_map/ppermute | solution.py:463
  11.3 1.3 %collective-permute-done.1 = s32[1,128]{1,0:T(1,128)S(1)} collective-permute-done((s32[1,128]{1,0:T(1,128)S(1)}, s32[1,128]{1,0:T(1,128)S(1)}, u32[]{:S(2)}, u32[]{:S(2)}) %collective-permute-start.1) | collective-permute-done | bytes 544 | tf_op jit(solution)/shard_map/ppermute | solution.py:463
  12.6 1.8 %collective-permute-start.2 = (s32[1,128]{1,0:T(1,128)S(1)}, s32[1,128]{1,0:T(1,128)S(1)}, u32[]{:S(2)}, u32[]{:S(2)}) collective-permute-start(s32[1,128]{1,0:T(1,128)S(1)} %add.31), channel_id=1, source_target_pairs={{0,5},{1,4},{2,7},{3,6},{4,1},{5,0},{6,3},{7,2},{8,13},{9,12},{10,... | collective-permute-start | bytes 1544 | tf_op jit(solution)/shard_map/ppermute | solution.py:463
  14.4 1.3 %collective-permute-done.2 = s32[1,128]{1,0:T(1,128)S(1)} collective-permute-done((s32[1,128]{1,0:T(1,128)S(1)}, s32[1,128]{1,0:T(1,128)S(1)}, u32[]{:S(2)}, u32[]{:S(2)}) %collective-permute-start.2) | collective-permute-done | bytes 544 | tf_op jit(solution)/shard_map/ppermute | solution.py:463
  15.7 2.7 %collective-permute-start.3 = (s32[1,128]{1,0:T(1,128)S(1)}, s32[1,128]{1,0:T(1,128)S(1)}, u32[]{:S(2)}, u32[]{:S(2)}) collective-permute-start(s32[1,128]{1,0:T(1,128)S(1)} %add.32), channel_id=1, source_target_pairs={{0,9},{1,8},{2,11},{3,10},{4,13},{5,12},{6,15},{7,14},{8,1},{9,0},... | collective-permute-start | bytes 1544 | tf_op jit(solution)/shard_map/ppermute | solution.py:463
  19.0 0.6 %collective-permute-done.3 = s32[1,128]{1,0:T(1,128)S(1)} collective-permute-done((s32[1,128]{1,0:T(1,128)S(1)}, s32[1,128]{1,0:T(1,128)S(1)}, u32[]{:S(2)}, u32[]{:S(2)}) %collective-permute-start.3) | collective-permute-done | bytes 544 | tf_op jit(solution)/shard_map/ppermute | solution.py:463
  19.7 0.0 collective-permute-done.4.other_ref
  19.7 0.0 copy-done
  19.7 0.2 slots.1
  19.9 1.6 %collective-permute-start.5 = (f32[2,56,128]{2,1,0:T(8,128)S(1)}, f32[2,56,128]{2,1,0:T(8,128)S(1)}, u32[]{:S(2)}, u32[]{:S(2)}) collective-permute-start(f32[2,56,128]{2,1,0:T(8,128)S(1)} %get-tuple-element.22), channel_id=1, source_target_pairs={{0,3},{1,2},{2,1},{3,0},{4,7},{5,6},{6,5},{7,4},{8,11},{9,10},{10,... | collective-permute-start | bytes 172040 | tf_op jit(solution)/shard_map/ppermute | solution.py:483
  21.5 1.3 %collective-permute-start.6 = (f32[2,56,128]{2,1,0:T(8,128)S(1)}, f32[2,56,128]{2,1,0:T(8,128)S(1)}, u32[]{:S(2)}, u32[]{:S(2)}) collective-permute-start(f32[2,56,128]{2,1,0:T(8,128)S(1)} %get-tuple-element.23), channel_id=1, source_target_pairs={{0,7},{1,6},{2,5},{3,4},{4,3},{5,2},{6,1},{7,0},{8,15},{9,14},{10,... | collective-permute-start | bytes 172040 | tf_op jit(solution)/shard_map/ppermute | solution.py:483
  22.8 0.1 collective-permute-start.7
  22.9 1.0 %collective-permute-done.5 = f32[2,56,128]{2,1,0:T(8,128)S(1)} collective-permute-done((f32[2,56,128]{2,1,0:T(8,128)S(1)}, f32[2,56,128]{2,1,0:T(8,128)S(1)}, u32[]{:S(2)}, u32[]{:S(2)}) %collective-permute-start.5) | collective-permute-done | bytes 57376 | tf_op jit(solution)/shard_map/ppermute | solution.py:483
  23.9 2.4 %collective-permute-done.6 = f32[2,56,128]{2,1,0:T(8,128)S(1)} collective-permute-done((f32[2,56,128]{2,1,0:T(8,128)S(1)}, f32[2,56,128]{2,1,0:T(8,128)S(1)}, u32[]{:S(2)}, u32[]{:S(2)}) %collective-permute-start.6) | collective-permute-done | bytes 57376 | tf_op jit(solution)/shard_map/ppermute | solution.py:483
  26.3 0.2 collective-permute-done.7
  26.5 2.6 %collective-permute-start.8 = (f32[1,56,128]{2,1,0:T(8,128)S(1)}, f32[1,56,128]{2,1,0:T(8,128)S(1)}, u32[]{:S(2)}, u32[]{:S(2)}) collective-permute-start(f32[1,56,128]{2,1,0:T(8,128)S(1)} %get-tuple-element.25), channel_id=1, source_target_pairs={{0,9},{1,8},{2,11},{3,10},{4,13},{5,12},{6,15},{7,14},{8,1},{9,0},... | collective-permute-start | bytes 86024 | tf_op jit(solution)/shard_map/ppermute | solution.py:487
  29.1 1.7 %collective-permute-done.8.refs_0_ = f32[1,56,128]{2,1,0:T(8,128)S(1)} collective-permute-done((f32[1,56,128]{2,1,0:T(8,128)S(1)}, f32[1,56,128]{2,1,0:T(8,128)S(1)}, u32[]{:S(2)}, u32[]{:S(2)}) %collective-permute-start.8) | collective-permute-done | bytes 28704 | tf_op jit(solution)/shard_map/ppermute | solution.py:487
  30.8 0.0 copy-done.1
  30.8 0.0 copy-done.2
  30.8 0.9 %brick.1 = f32[1,4,2304]{2,1,0:T(4,128)} custom-call(f32[1,56,128]{2,1,0:T(8,128)S(1)} %get-tuple-element.26.mine_ref, f32[1,56,128]{2,1,0:T(8,128)S(1)} %collective-permute-done.8.refs_0_, f32[4,640]{1,0:T(4,128)S(1)} %copy-done.1, f32[4,640]{1,0:T(4,128)S(1)} %copy-done.2), custom_call_target="tpu_custom_call" | custom-call | tf_op jit(solution)/shard_map/brick/pallas_call | solution.py:418
  (6 shorter events, 0.0 us)
Async XLA Ops:
  5.0 14.7 %copy-start = (f32[16,56,128]{2,1,0:T(8,128)S(1)}, f32[16,56,128]{2,1,0:T(8,128)}, u32[]{:S(2)}) copy-start(f32[16,56,128]{2,1,0:T(8,128)} %constant.6.clone.window_ref) | copy-start | bytes 1376260
  6.2 24.5 %copy-start.1 = (f32[4,640]{1,0:T(4,128)S(1)}, f32[4,640]{1,0:T(4,128)}, u32[]{:S(2)}) copy-start(f32[4,640]{1,0:T(4,128)} %constant.7.clone.refs_1_) | copy-start | bytes 30724
  6.2 24.5 %copy-start.2 = (f32[4,640]{1,0:T(4,128)S(1)}, f32[4,640]{1,0:T(4,128)}, u32[]{:S(2)}) copy-start(f32[4,640]{1,0:T(4,128)} %constant.8.clone.refs_2_) | copy-start | bytes 30724
  6.2 13.4 %collective-permute-start.4 = (f32[16,56,128]{2,1,0:T(8,128)S(1)}, f32[16,56,128]{2,1,0:T(8,128)S(1)}, u32[]{:S(2)}, u32[]{:S(2)}) collective-permute-start(f32[16,56,128]{2,1,0:T(8,128)S(1)} %shard_map.110.mine_ref), channel_id=1, source_target_pairs={{0,1},{1,0},{2,3},{3,2},{4,5},{5,4},{6,7},{7,6},{8,9},{9,8},{10,11... | collective-permute-start | bytes 1376264 | tf_op jit(solution)/shard_map/ppermute | solution.py:481
  7.5 1.2 %collective-permute-start = (s32[1,128]{1,0:T(1,128)S(1)}, s32[1,128]{1,0:T(1,128)S(1)}, u32[]{:S(2)}, u32[]{:S(2)}) collective-permute-start(s32[1,128]{1,0:T(1,128)S(1)} %seed.1), channel_id=1, source_target_pairs={{0,1},{1,0},{2,3},{3,2},{4,5},{5,4},{6,7},{7,6},{8,9},{9,8},{10,11... | collective-permute-start | bytes 1544 | tf_op jit(solution)/shard_map/ppermute | solution.py:463
  8.7 3.9 %collective-permute-start.1 = (s32[1,128]{1,0:T(1,128)S(1)}, s32[1,128]{1,0:T(1,128)S(1)}, u32[]{:S(2)}, u32[]{:S(2)}) collective-permute-start(s32[1,128]{1,0:T(1,128)S(1)} %add.30), channel_id=1, source_target_pairs={{0,3},{1,2},{2,1},{3,0},{4,7},{5,6},{6,5},{7,4},{8,11},{9,10},{10,... | collective-permute-start | bytes 1544 | tf_op jit(solution)/shard_map/ppermute | solution.py:463
  12.6 3.0 %collective-permute-start.2 = (s32[1,128]{1,0:T(1,128)S(1)}, s32[1,128]{1,0:T(1,128)S(1)}, u32[]{:S(2)}, u32[]{:S(2)}) collective-permute-start(s32[1,128]{1,0:T(1,128)S(1)} %add.31), channel_id=1, source_target_pairs={{0,5},{1,4},{2,7},{3,6},{4,1},{5,0},{6,3},{7,2},{8,13},{9,12},{10,... | collective-permute-start | bytes 1544 | tf_op jit(solution)/shard_map/ppermute | solution.py:463
  15.7 4.0 %collective-permute-start.3 = (s32[1,128]{1,0:T(1,128)S(1)}, s32[1,128]{1,0:T(1,128)S(1)}, u32[]{:S(2)}, u32[]{:S(2)}) collective-permute-start(s32[1,128]{1,0:T(1,128)S(1)} %add.32), channel_id=1, source_target_pairs={{0,9},{1,8},{2,11},{3,10},{4,13},{5,12},{6,15},{7,14},{8,1},{9,0},... | collective-permute-start | bytes 1544 | tf_op jit(solution)/shard_map/ppermute | solution.py:463
  19.9 4.0 %collective-permute-start.5 = (f32[2,56,128]{2,1,0:T(8,128)S(1)}, f32[2,56,128]{2,1,0:T(8,128)S(1)}, u32[]{:S(2)}, u32[]{:S(2)}) collective-permute-start(f32[2,56,128]{2,1,0:T(8,128)S(1)} %get-tuple-element.22), channel_id=1, source_target_pairs={{0,3},{1,2},{2,1},{3,0},{4,7},{5,6},{6,5},{7,4},{8,11},{9,10},{10,... | collective-permute-start | bytes 172040 | tf_op jit(solution)/shard_map/ppermute | solution.py:483
  21.5 4.8 %collective-permute-start.6 = (f32[2,56,128]{2,1,0:T(8,128)S(1)}, f32[2,56,128]{2,1,0:T(8,128)S(1)}, u32[]{:S(2)}, u32[]{:S(2)}) collective-permute-start(f32[2,56,128]{2,1,0:T(8,128)S(1)} %get-tuple-element.23), channel_id=1, source_target_pairs={{0,7},{1,6},{2,5},{3,4},{4,3},{5,2},{6,1},{7,0},{8,15},{9,14},{10,... | collective-permute-start | bytes 172040 | tf_op jit(solution)/shard_map/ppermute | solution.py:483
  22.8 3.7 %collective-permute-start.7 = (f32[2,56,128]{2,1,0:T(8,128)S(1)}, f32[2,56,128]{2,1,0:T(8,128)S(1)}, u32[]{:S(2)}, u32[]{:S(2)}) collective-permute-start(f32[2,56,128]{2,1,0:T(8,128)S(1)} %get-tuple-element.24), channel_id=1, source_target_pairs={{0,5},{1,4},{2,7},{3,6},{4,1},{5,0},{6,3},{7,2},{8,13},{9,12},{10,... | collective-permute-start | bytes 172040 | tf_op jit(solution)/shard_map/ppermute | solution.py:483
  26.5 4.3 %collective-permute-start.8 = (f32[1,56,128]{2,1,0:T(8,128)S(1)}, f32[1,56,128]{2,1,0:T(8,128)S(1)}, u32[]{:S(2)}, u32[]{:S(2)}) collective-permute-start(f32[1,56,128]{2,1,0:T(8,128)S(1)} %get-tuple-element.25), channel_id=1, source_target_pairs={{0,9},{1,8},{2,11},{3,10},{4,13},{5,12},{6,15},{7,14},{8,1},{9,0},... | collective-permute-start | bytes 86024 | tf_op jit(solution)/shard_map/ppermute | solution.py:487
